TPU v7x, 128 devices: a whole 4x4x4 slice. The times are simulated.
128 devices in a mesh: rows: 64 (over y, x, z), grp: 2 (over core).
Axes of the slice: x: 4, y: 4, z: 4, core: 2. Of those that a mesh axis runs over, the one named last changes fastest.
Arguments:
- snap_early: float32 [12288, 128, 128], P(('rows', 'grp')), as said below
- snap_late: float32 [12288, 128, 128], P(('rows', 'grp')), as said below
- block_ids: int32 [12288], P(('rows', 'grp')), may hold values from 0 to 12287, as said below
- block_owner: int32 [12288], replicated, may hold values from 0 to 127, as said below
- block_slot: int32 [12288], replicated, may hold values from 0 to 127, as said below
Outputs:
- modes: float32 [16384, 128, 128], P(('rows', 'grp'))
- operator: float32 [128, 128], replicated
Inputs may be any that keep to these rules, and one draw needn't show every extreme that they name: block_ids is a permutation of 0 to 12287. `block_owner`: each analysis device owns at most 128 blocks and one owns exactly 128; among the blocks of one solver device (aligned runs of 96 slots of block_ids) at most 1 go to one analysis device, and in every draw some solver device sends exactly 1 to one. `block_slot`: the blocks of one analysis device take the slots 0 to c - 1, each once, where c is their count. `snap_early`: Real-valued snapshots with magnitudes from below one to some thousands, row and column scales spread by up to a factor of about 900; the matrix of all rows has full column rank. `snap_late`: Real-valued snapshots, the early ones advanced by one step of a linear flow plus noise.
All inputs are finite; a program needn't handle non-finite values.
Results may differ from a plain program's by a relative error of at most 0.0003.
Values sent between devices are 32-bit elements; how exact they have to be, the bound alone decides.
No kernel may reach another device: no remote copies, remote signals or barrier semaphores. Data moves between devices by JAX's collectives and lax.ppermute only.
A program may use at most 128 MiB of HBM per device.

v0:
```python
import jax
import jax.numpy as jnp
from jax import lax
from jax.sharding import PartitionSpec as P

CAP = 128


def swapped(value, axis, stride):
    return lax.ppermute(value, axis, [(i, i ^ 1 << stride) for i in range(lax.axis_size(axis))])


def upper_factor(gram_total):
    order = gram_total.shape[0]
    index = jnp.arange(order, dtype=jnp.int32)

    def step(j, factor):
        column = lax.dynamic_slice_in_dim(factor, j, 1, 1)[:, 0]
        grow = lax.dynamic_slice_in_dim(gram_total, j, 1, 0)[0]
        rest = grow - jnp.dot(column, factor, precision=lax.Precision.HIGHEST)
        pivot = jnp.sqrt(jnp.sum(jnp.where(index == j, rest, 0.0)))
        newrow = jnp.where(index >= j, rest / pivot, 0.0)
        picked = (index == j).astype(gram_total.dtype)
        return factor + picked[:, None] * newrow[None, :]

    return lax.fori_loop(0, order, step, jnp.zeros_like(gram_total))


def upper_inverse(factor):
    order = factor.shape[0]
    index = jnp.arange(order, dtype=jnp.int32)

    def step(t, inverse):
        i = order - 1 - t
        frow = lax.dynamic_slice_in_dim(factor, i, 1, 0)[0]
        unit = (index == i).astype(factor.dtype)
        diagonal = jnp.sum(frow * unit)
        newrow = (unit - jnp.dot(frow, inverse, precision=lax.Precision.HIGHEST)) / diagonal
        return inverse + unit[:, None] * newrow[None, :]

    return lax.fori_loop(0, order, step, jnp.zeros_like(factor))


def gram_pair(early_blocks, late_blocks):
    early_rows = early_blocks.reshape((-1, early_blocks.shape[-1]))
    late_rows = late_blocks.reshape((-1, late_blocks.shape[-1]))
    gram_local = jnp.einsum("rk,rl->kl", early_rows, early_rows, precision=lax.Precision.HIGHEST)
    cross_local = jnp.einsum("rk,rl->kl", early_rows, late_rows, precision=lax.Precision.HIGHEST)
    return jnp.stack([gram_local, cross_local])


def combine_stats(stacked):
    members = lax.axis_size(("rows", "grp"))
    for bit_index in range(members.bit_length() - 1):
        stacked = stacked + swapped(stacked, ("rows", "grp"), bit_index)
    return stacked


def finish(stacked, row_total):
    gram_total = stacked[0] / row_total
    cross_total = stacked[1] / row_total
    inverse = upper_inverse(upper_factor(gram_total))
    coupled = jnp.dot(cross_total, inverse, precision=lax.Precision.HIGHEST)
    operator = jnp.dot(inverse.T, coupled, precision=lax.Precision.HIGHEST)
    return (inverse, operator)


def apply_inverse(late_blocks, inverse):
    late_rows = late_blocks.reshape((-1, late_blocks.shape[-1]))
    solved = jnp.dot(late_rows, inverse, precision=lax.Precision.HIGHEST)
    return solved.reshape(late_blocks.shape)


def select_rows(matches, member):
    flat = member.reshape((member.shape[0], -1))
    chosen = jnp.dot(matches.astype(member.dtype), flat, precision=lax.Precision.HIGHEST)
    return chosen.reshape((matches.shape[0],) + member.shape[1:])


def arrange(values, destination, slot_here, slot_count):
    target = jnp.arange(slot_count, dtype=jnp.int32)
    matches = destination[None, :] == target[:, None]
    usable = jnp.any(matches, axis=1)
    picked = tuple((select_rows(matches, member) for member in values))
    carried = jnp.sum(jnp.where(matches, slot_here[None, :], 0), axis=1)
    slot_sent = jnp.where(usable, carried, -1)
    return picked + (slot_sent,)


def settle(values, slot_arrived, slot_count):
    target = jnp.arange(slot_count, dtype=jnp.int32)
    matches = slot_arrived[None, :] == target[:, None]
    return tuple((select_rows(matches, member) for member in values))


def deliver(payload):
    return lax.all_to_all(payload, ("rows", "grp"), split_axis=0, concat_axis=0, tiled=True)


def body(snap_early, snap_late, block_ids, block_owner, block_slot):
    members = lax.axis_size(("rows", "grp"))
    per_peer = (CAP + members - 1) // members
    row_total = snap_early.shape[0] * snap_early.shape[1] * members
    labels = jnp.arange(block_owner.shape[0], dtype=jnp.int32)
    hits = block_ids[:, None] == labels[None, :]
    owner_here = jnp.sum(jnp.where(hits, block_owner[None, :], 0), axis=1)
    slot_here = jnp.sum(jnp.where(hits, block_slot[None, :], 0), axis=1)
    destination = owner_here * per_peer + slot_here // members
    inverse, operator = finish(combine_stats(gram_pair(snap_early, snap_late)), row_total)
    payload = arrange(
        (apply_inverse(snap_late, inverse),), destination, slot_here, members * per_peer
    )
    arrived = deliver(payload)
    mode_blocks = settle(arrived[:1], arrived[1], CAP)[0]
    return (mode_blocks, operator)


def solution(mesh):
    placed = (
        P(("rows", "grp"), None, None),
        P(("rows", "grp"), None, None),
        P(("rows", "grp")),
        P(),
        P(),
    )
    return jax.shard_map(
        body,
        mesh=mesh,
        in_specs=placed,
        out_specs=(P(("rows", "grp"), None, None), P()),
        check_vma=False,
    )
```

profile of v0, /device:TPU:1, one launch (start us, length us, event | category | flops | bytes accessed | tf_op | source)
XLA Modules:
  0.0 687.2 jit_solution(6458417094833446998)
XLA Ops:
  0.7 13.4 %convolution_bitcast_fusion.4 = f32[1,128,128]{2,1,0:T(8,128)S(1)} fusion(f32[96,128,128]{2,1,0:T(8,128)} %param.9), kind=kOutput, calls=%fused_computation.35 | convolution fusion | flops 2415919104 | bytes 6356992 | tf_op jit(solution)/shard_map/rk,rl->kl/dot_general | solution.py:47
  14.1 10.0 %convolution_bitcast_fusion.3 = f32[1,128,128]{2,1,0:T(8,128)S(1)} fusion(f32[96,128,128]{2,1,0:T(8,128)S(1)} %copy-done, f32[96,128,128]{2,1,0:T(8,128)S(1)} %copy-done.1), kind=kOutput, calls=%fused_computation.34 | convolution fusion | flops 2415919104 | bytes 12648448 | tf_op jit(solution)/shard_map/rk,rl->kl/dot_general | solution.py:48
  24.2 1.5 collective-permute-start
  25.6 1.0 collective-permute-done
  26.6 1.8 collective-permute-start.1
  28.5 3.5 collective-permute-done.1
  32.0 3.2 collective-permute-start.2
  35.2 2.7 collective-permute-done.2
  37.9 1.7 collective-permute-start.3
  39.6 1.7 select_reduce_fusion
  42.2 2.8 collective-permute-start.4
  45.1 3.0 collective-permute-done.4
  48.1 1.4 collective-permute-start.5
  49.7 2.3 collective-permute-done.5
  52.0 3.0 collective-permute-start.6
  55.7 14.4 %all-to-all-start = ((s32[128,1,1]{2,1,0:T(1,128)}), s32[128,1,1]{2,1,0:T(1,128)S(1)}, u32[]{:S(2)}, u32[]{:S(2)}) async-start(s32[128,1,1]{2,1,0:T(1,128)} %copy.36), calls=%async_computation | async-start | bytes 131072 | tf_op jit(solution)/shard_map/all_to_all | solution.py:97
  70.3 229.2 %while.32 = (s32[]{:T(128)}, f32[128,128]{0,1:T(8,128)S(1)}, f32[128,128]{1,0:T(8,128)S(1)}, s32[]{:T(128)}, s32[]{:T(128)}) while((s32[]{:T(128)}, f32[128,128]{0,1:T(8,128)S(1)}, f32[128,128]{1,0:T(8,128)S(1)}, s32[]{:T(128)}, s32[]{:T(128)}) %tuple.88), condition=%wide.region_6.7_spmd.clone.clone, body=%wide.region_4.6_spmd.clone.clone.sunk | while | flops 263298 | bytes 333416 | solution.py:26
  70.3 0.9 fusion.60
  72.1 0.9 fusion.60
  75.7 0.9 fusion.60
  77.5 0.9 fusion.60
  81.0 0.9 fusion.60
  82.8 0.9 fusion.60
  86.4 0.9 fusion.60
  88.2 0.9 fusion.60
  93.6 0.9 fusion.60
  98.9 0.9 fusion.60
  100.7 0.9 fusion.60
  104.3 0.9 fusion.60
  106.1 0.9 fusion.60
  109.7 0.9 fusion.60
  111.5 0.9 fusion.60
  115.1 0.9 fusion.60
  116.8 0.9 fusion.60
  120.4 0.9 fusion.60
  299.5 213.8 %while.31 = (s32[]{:T(128)}, f32[128,128]{1,0:T(8,128)S(1)}, f32[128,128]{1,0:T(8,128)S(1)}, s32[]{:T(128)}, s32[]{:T(128)}, /*index=5*/s32[]{:T(128)}, s32[]{:T(128)}) while((s32[]{:T(128)}, f32[128,128]{1,0:T(8,128)S(1)}, f32[128,128]{1,0:T(8,128)S(1)}, s32[]{:T(128)}, s32[]{:T(128)}, /*index=5*/s32[]{:T(128)}, s32[]{:T(128)}) %tuple.91), condition=%wide.region_9.10_spmd.clone, body=%wide.region_7.9_spmd.clone.sunk | while | flops 263302 | bytes 199850 | solution.py:41
  513.4 9.2 %convolution_bitcast_fusion.2 = f32[12288,128]{0,1:T(8,128)} fusion(f32[128,128]{1,0:T(8,128)S(1)} %get-tuple-element.195, f32[12288,128]{1,0:T(8,128)} %bitcast.73), kind=kOutput, calls=%fused_computation.25 | convolution fusion | flops 2415919104 | bytes 12648448 | tf_op jit(solution)/shard_map/dot_general | solution.py:70
  522.6 6.6 copy.40
  529.2 7.1 %reshape_reshape.3 = f32[96,16384]{1,0:T(8,128)} reshape(f32[12288,128]{1,0:T(8,128)} %copy.40) | data formatting | bytes 12582912 | tf_op jit(solution)/shard_map/reshape;reshape | solution.py:75
  536.3 6.1 fusion.18
  542.4 8.3 %copy.42 = f32[128,128,128]{2,1,0:T(8,128)} copy(f32[128,128,128]{2,0,1:T(8,128)S(1)} %fusion.18) | data formatting | bytes 16777216 | tf_op jit(solution)/shard_map/dot_general | solution.py:76
  550.7 10.6 %all-to-all-start.1 = ((f32[128,128,128]{2,1,0:T(8,128)}), f32[128,128,128]{2,1,0:T(8,128)}, u32[]{:S(2)}, u32[]{:S(2)}) async-start(f32[128,128,128]{2,1,0:T(8,128)} %copy.42), calls=%async_computation.1 | async-start | bytes 16777216 | tf_op jit(solution)/shard_map/all_to_all | solution.py:97
  561.2 2.4 reduce
  563.8 0.9 fusion.36
  564.7 97.6 %all-to-all-done.1 = f32[128,128,128]{2,1,0:T(8,128)} async-done(((f32[128,128,128]{2,1,0:T(8,128)}), f32[128,128,128]{2,1,0:T(8,128)}, u32[]{:S(2)}, u32[]{:S(2)}) %all-to-all-start.1) | async-done | bytes 8388640 | tf_op jit(solution)/shard_map/all_to_all | solution.py:97
  662.3 9.3 %copy.43 = f32[128,128,128]{0,2,1:T(8,128)} copy(f32[128,128,128]{2,1,0:T(8,128)} %all-to-all-done.1) | data formatting | bytes 16777216 | tf_op jit(solution)/shard_map/all_to_all | solution.py:97
  671.6 7.1 %fusion.16 = f32[128,128,128]{2,0,1:T(8,128)S(1)} fusion(f32[128,128,128]{0,2,1:T(8,128)} %copy.43, s32[128]{0:T(128)S(1)} %reduce), kind=kOutput, calls=%fused_computation.26 | convolution fusion | flops 3221241856 | bytes 16777728 | tf_op jit(solution)/shard_map/dot_general | solution.py:76
  678.7 8.3 %copy.44 = f32[128,128,128]{2,1,0:T(8,128)} copy(f32[128,128,128]{2,0,1:T(8,128)S(1)} %fusion.16) | data formatting | bytes 16777216
  (1165 shorter events, 323.9 us)
Async XLA Ops:
  0.6 13.4 %copy-start = (f32[96,128,128]{2,1,0:T(8,128)S(1)}, f32[96,128,128]{2,1,0:T(8,128)}, u32[]{:S(2)}) copy-start(f32[96,128,128]{2,1,0:T(8,128)} %param.9) | copy-start | bytes 18874372
  0.6 13.4 %copy-start.1 = (f32[96,128,128]{2,1,0:T(8,128)S(1)}, f32[96,128,128]{2,1,0:T(8,128)}, u32[]{:S(2)}) copy-start(f32[96,128,128]{2,1,0:T(8,128)} %param.10) | copy-start | bytes 18874372
  14.1 25.5 %copy-start.2 = (s32[12288]{0:T(1024)S(1)}, s32[12288]{0:T(1024)}, u32[]{:S(2)}) copy-start(s32[12288]{0:T(1024)} %param.13) | copy-start | bytes 147460
  14.1 25.5 %copy-start.3 = (s32[12288]{0:T(1024)S(1)}, s32[12288]{0:T(1024)}, u32[]{:S(2)}) copy-start(s32[12288]{0:T(1024)} %param.12) | copy-start | bytes 147460
  14.1 25.5 %copy-start.4 = (s32[96]{0:T(128)S(1)}, s32[96]{0:T(128)}, u32[]{:S(2)}) copy-start(s32[96]{0:T(128)} %param.11) | copy-start | bytes 1156
  24.2 2.4 collective-permute-start
  26.6 5.3 collective-permute-start.1
  32.0 5.9 collective-permute-start.2
  37.9 4.3 collective-permute-start.3
  42.2 5.8 collective-permute-start.4
  48.1 3.9 collective-permute-start.5
  52.0 18.2 %collective-permute-start.6 = (f32[2,128,128]{2,1,0:T(8,128)S(1)}, f32[2,128,128]{2,1,0:T(8,128)S(1)}, u32[]{:S(2)}, u32[]{:S(2)}) collective-permute-start(f32[2,128,128]{2,1,0:T(8,128)S(1)} %add.108), channel_id=1, source_target_pairs={{0,64},{1,65},{2,66},{3,67},{4,68},{5,69},{6,70},{7,71},{8,72},{9,... | collective-permute-start | bytes 393224 | tf_op jit(solution)/shard_map/ppermute | solution.py:10
  55.7 494.9 %all-to-all-start = ((s32[128,1,1]{2,1,0:T(1,128)}), s32[128,1,1]{2,1,0:T(1,128)S(1)}, u32[]{:S(2)}, u32[]{:S(2)}) async-start(s32[128,1,1]{2,1,0:T(1,128)} %copy.36), calls=%async_computation | async-start | bytes 131072 | tf_op jit(solution)/shard_map/all_to_all | solution.py:97
  550.7 111.7 %all-to-all-start.1 = ((f32[128,128,128]{2,1,0:T(8,128)}), f32[128,128,128]{2,1,0:T(8,128)}, u32[]{:S(2)}, u32[]{:S(2)}) async-start(f32[128,128,128]{2,1,0:T(8,128)} %copy.42), calls=%async_computation.1 | async-start | bytes 16777216 | tf_op jit(solution)/shard_map/all_to_all | solution.py:97
where the time goes:
time: 697 us; the launch traced here: 687 us
  matrix products  270 us (39%)
  other arithmetic  119 us (17%)
  waiting for transfers between devices  111 us (16%)
  loops' own time  105 us (15%)
  local copies, waits for them, and re-layouts  40.4 us (6%)
  starting transfers between devices  40.4 us (6%)
    dot_general x128, matrix products, step(): rest = grow - jnp.dot(column, factor, precision=lax.Precision.HIGHEST)  116 us
    dot_general x128, matrix products, step(): jnp.dot(frow, inverse, precision=lax.Precision.HIGHEST)  108 us
    another operation x1, loops' own time, upper_factor(): return lax.fori_loop(0, order, step, jnp.zeros_like(gram_total))  100 us
    all_to_all x2, waiting for transfers between devices, deliver(): lax.all_to_all(payload, ('rows', 'grp'), split_axis=0, concat_axis=0, til...  97.6 us
    reduce_sum x128, other arithmetic, step(): diagonal = jnp.sum(frow * unit)  87.9 us
    all_to_all x2, starting transfers between devices, deliver(): lax.all_to_all(payload, ('rows', 'grp'), split_axis=0, concat_axis=0, til...  25 us
    ppermute x7, starting transfers between devices, swapped(): lax.ppermute(value, axis, [(i, i ^ 1 << stride) for i in range(lax.axis_s...  15.4 us
  transfers between devices with their start and end apart: 9, of which 7 were waited for; matrix products, arithmetic and copies ran while one was open for 55% of the time, Pallas kernels for 0%

commit v1 on v0

v1 whole, which is shorter than its diff:
```python
import functools

import jax
import jax.numpy as jnp
from jax import lax
from jax.experimental import pallas as pl
from jax.experimental.pallas import tpu as pltpu
from jax.sharding import PartitionSpec as P

AXES = ("rows", "grp")
CHUNKS = 2
GRAM_STEP = 8
ROWS = 8
APPLY_STEP = 16


def split_pair(x):
    hi = x.astype(jnp.bfloat16)
    lo = (x - hi.astype(jnp.float32)).astype(jnp.bfloat16)
    return hi, lo


def contract_rows(a, b):
    return lax.dot_general(
        a, b, (((0,), (0,)), ((), ())), preferred_element_type=jnp.float32
    )


def pack_kernel(height, lo, dest_ref, late_ref, out_ref, buf, sem_in, sem_out):
    count = late_ref.shape[0]

    def load(i):
        return pltpu.make_async_copy(
            late_ref.at[i, pl.ds(lo, height)], buf.at[dest_ref[i]], sem_in
        )

    def start(i, carry):
        load(i).start()
        return carry

    lax.fori_loop(0, count, start, 0)
    pltpu.make_async_copy(
        late_ref.at[pl.ds(0, count), pl.ds(lo, height)], buf.at[pl.ds(0, count)], sem_in
    ).wait()
    out = pltpu.make_async_copy(buf, out_ref, sem_out)
    out.start()
    out.wait()


def pack(late, dest, members, lo, height):
    width = late.shape[2]
    return pl.pallas_call(
        functools.partial(pack_kernel, height, lo),
        grid_spec=pltpu.PrefetchScalarGridSpec(
            num_scalar_prefetch=1,
            grid=(1,),
            in_specs=[pl.BlockSpec(memory_space=pl.ANY)],
            out_specs=pl.BlockSpec(memory_space=pl.ANY),
            scratch_shapes=[
                pltpu.VMEM((members, height, width), jnp.float32),
                pltpu.SemaphoreType.DMA,
                pltpu.SemaphoreType.DMA,
            ],
        ),
        out_shape=jax.ShapeDtypeStruct((members, height, width), jnp.float32),
        cost_estimate=pl.CostEstimate(flops=100000000, bytes_accessed=1 << 23, transcendentals=0),
        name="pack",
    )(dest, late)


def gram_kernel(note_ref, early_ref, late_ref, out_ref, acc):
    step = pl.program_id(0)

    @pl.when(step == 0)
    def _():
        acc[...] = jnp.zeros_like(acc)

    width = early_ref.shape[2]
    early = early_ref[...].reshape((-1, width))
    late = late_ref[...].reshape((-1, width))
    ehi, elo = split_pair(early)
    lhi, llo = split_pair(late)
    acc[...] += contract_rows(
        jnp.concatenate([ehi, lhi, llo], axis=1), jnp.concatenate([ehi, elo], axis=1)
    )

    @pl.when(step == pl.num_programs(0) - 1)
    def _():
        mixed = acc[0:width, width:]
        gram = acc[0:width, 0:width] + (mixed + mixed.T)
        flipped = (
            acc[width : 2 * width, 0:width]
            + acc[width : 2 * width, width:]
            + acc[2 * width :, 0:width]
        )
        out_ref[...] = jnp.zeros_like(out_ref)
        out_ref[:, 0, :] = gram
        out_ref[:, 1, :] = flipped.T
        out_ref[:, 2, :] = note_ref[...]


def gram_pair(note, early, late):
    count, block, width = early.shape
    spec = pl.BlockSpec((GRAM_STEP, block, width), lambda i: (i, 0, 0))
    flops = 2 * count * block * 6 * width * width
    return pl.pallas_call(
        gram_kernel,
        grid=(count // GRAM_STEP,),
        in_specs=[pl.BlockSpec(note.shape, lambda i: (0, 0)), spec, spec],
        out_specs=pl.BlockSpec((width, ROWS, width), lambda i: (0, 0, 0)),
        out_shape=jax.ShapeDtypeStruct((width, ROWS, width), jnp.float32),
        scratch_shapes=[pltpu.VMEM((3 * width, 2 * width), jnp.float32)],
        cost_estimate=pl.CostEstimate(flops=flops, bytes_accessed=1 << 23, transcendentals=0),
        name="gram",
    )(note, early, late)


def dot3(a, b):
    return jnp.dot(a, b, precision=lax.Precision.HIGHEST, preferred_element_type=jnp.float32)


def finish_kernel(row_total, stats_ref, weight_ref, operator_ref, work):
    order = stats_ref.shape[0]
    row_id = lax.broadcasted_iota(jnp.int32, (order, 1), 0)
    lane = lax.broadcasted_iota(jnp.int32, (1, 2 * order), 1)
    lane_half = lax.broadcasted_iota(jnp.int32, (1, order), 1)
    work[:, 0:order] = stats_ref[:, 0, :] / row_total
    work[:, order:] = (row_id == lane_half).astype(jnp.float32)

    def step(j, carry):
        row = work[pl.ds(j, 1), :]
        inv = lax.rsqrt(jnp.sum(jnp.where(lane == j, row, 0.0), axis=1, keepdims=True))
        scaled = row * inv
        table = work[...]
        column = jnp.sum(
            jnp.where(lane_half == j, table[:, 0:order], 0.0), axis=1, keepdims=True
        )
        down = jnp.where(row_id > j, column * inv, 0.0)
        work[...] = jnp.where(row_id == j, scaled, table - down * scaled)
        return carry

    lax.fori_loop(0, order, step, 0)
    inverse_t = work[:, order:]
    inverse = inverse_t.T
    cross = stats_ref[:, 1, :] / row_total
    operator_ref[...] = dot3(inverse_t, dot3(cross, inverse))
    whi, wlo = split_pair(inverse)
    weight_ref[0:order, 0:order] = whi
    weight_ref[0:order, order:] = wlo
    weight_ref[order:, 0:order] = whi
    weight_ref[order:, order:] = wlo


def finish(stats, row_total):
    order = stats.shape[0]
    return pl.pallas_call(
        functools.partial(finish_kernel, float(row_total)),
        out_shape=(
            jax.ShapeDtypeStruct((2 * order, 2 * order), jnp.bfloat16),
            jax.ShapeDtypeStruct((order, order), jnp.float32),
        ),
        scratch_shapes=[pltpu.VMEM((order, 2 * order), jnp.float32)],
        cost_estimate=pl.CostEstimate(flops=1000000000, bytes_accessed=1 << 19, transcendentals=0),
        name="finish",
    )(stats)


def apply_kernel(lo, place_ref, weight_ref, arrived_ref, *rest):
    out_ref, buf_in, buf_out, sem_in, sem_out = rest[-5:]
    count, height, width = arrived_ref.shape
    steps = count // APPLY_STEP

    def fetch(t, k):
        return pltpu.make_async_copy(
            arrived_ref.at[pl.ds(t * APPLY_STEP, APPLY_STEP)], buf_in.at[k], sem_in.at[k]
        )

    def drain(k):
        pltpu.make_async_copy(
            buf_out.at[k], out_ref.at[pl.ds(0, APPLY_STEP), pl.ds(lo, height)], sem_out.at[k]
        ).wait()

    fetch(0, 0).start()

    def step(t, carry):
        k = lax.rem(t, 2)

        @pl.when(t + 1 < steps)
        def _():
            fetch(t + 1, 1 - k).start()

        fetch(t, k).wait()

        @pl.when(t >= 2)
        def _():
            drain(k)

        rows = buf_in[k].reshape((APPLY_STEP * height, width))
        hi, lo_part = split_pair(rows)
        wide = jnp.dot(
            jnp.concatenate([hi, lo_part], axis=1),
            weight_ref[...],
            preferred_element_type=jnp.float32,
        )
        solved = wide[:, 0:width] + wide[:, width:]
        buf_out[k] = solved.reshape((APPLY_STEP, height, width))
        for i in range(APPLY_STEP):
            code = place_ref[t * APPLY_STEP + i]
            slot = jnp.bitwise_and(code, 127)

            @pl.when(code >= 128)
            def _():
                buf_out[k, i] = jnp.zeros((height, width), jnp.float32)

            pltpu.make_async_copy(
                buf_out.at[k, i], out_ref.at[slot, pl.ds(lo, height)], sem_out.at[k]
            ).start()
        return carry

    lax.fori_loop(0, steps, step, 0)
    drain(0)
    drain(1)


def apply_inverse(place, weight, arrived, modes, lo, block):
    count, height, width = arrived.shape
    whole = pl.BlockSpec(memory_space=pltpu.VMEM)
    anywhere = pl.BlockSpec(memory_space=pl.ANY)
    args = (place, weight, arrived) + (() if modes is None else (modes,))
    return pl.pallas_call(
        functools.partial(apply_kernel, lo),
        grid_spec=pltpu.PrefetchScalarGridSpec(
            num_scalar_prefetch=1,
            grid=(1,),
            in_specs=[whole, anywhere] + ([] if modes is None else [anywhere]),
            out_specs=anywhere,
            scratch_shapes=[
                pltpu.VMEM((2, APPLY_STEP, height, width), jnp.float32),
                pltpu.VMEM((2, APPLY_STEP, height, width), jnp.float32),
                pltpu.SemaphoreType.DMA((2,)),
                pltpu.SemaphoreType.DMA((2,)),
            ],
        ),
        out_shape=jax.ShapeDtypeStruct((count, block, width), jnp.float32),
        input_output_aliases={} if modes is None else {3: 0},
        cost_estimate=pl.CostEstimate(
            flops=8 * count * height * width * width, bytes_accessed=1 << 23, transcendentals=0
        ),
        name="apply",
    )(*args)


def exchange(payload):
    return lax.all_to_all(payload, AXES, split_axis=0, concat_axis=0, tiled=True)


def body(snap_early, snap_late, block_ids, block_owner, block_slot):
    members = lax.axis_size(AXES)
    count, block, width = snap_late.shape
    row_total = count * block * members
    labels = jnp.arange(block_owner.shape[0], dtype=jnp.int32)
    code = block_owner * 128 + block_slot
    hits = block_ids[:, None] == labels[None, :]
    code_here = jnp.sum(jnp.where(hits, code[None, :], 0), axis=1)
    dest = code_here // 128
    slot_here = code_here % 128
    height = block // CHUNKS
    sent = [
        exchange(pack(snap_late, dest, members, c * height, height)) for c in range(CHUNKS)
    ]
    target = jnp.arange(members, dtype=jnp.int32)
    note = jnp.sum(
        jnp.where(dest[None, :] == target[:, None], slot_here[None, :] + 1, 0), axis=1
    )
    note = jnp.broadcast_to(note.astype(jnp.float32)[:, None], (members, width))
    partial = exchange(gram_pair(note, snap_early, snap_late))
    mine = jnp.sum(partial, axis=0)
    stats = exchange(jnp.broadcast_to(mine[None], (members, ROWS, width)))
    weight, operator = finish(stats, row_total)
    slot_in = partial[:, 2, 0].astype(jnp.int32)
    empty = slot_in == 0
    filled = jnp.sum((slot_in > 0).astype(jnp.int32))
    earlier = jnp.sum(
        jnp.where(empty[None, :] & (target[None, :] < target[:, None]), 1, 0), axis=1
    )
    place = jnp.where(empty, filled + earlier + 128, slot_in - 1)
    modes = None
    for c in range(CHUNKS):
        modes = apply_inverse(place, weight, sent[c], modes, c * height, block)
    return (modes, operator)


def solution(mesh):
    placed = (
        P(AXES, None, None),
        P(AXES, None, None),
        P(AXES),
        P(),
        P(),
    )
    return jax.shard_map(
        body,
        mesh=mesh,
        in_specs=placed,
        out_specs=(P(AXES, None, None), P()),
        check_vma=False,
    )
```

time: 697 us -> 187 us (0.27); the launches traced: 687 us -> 186 us
  matrix products: 270 us -> 0 us
  other arithmetic: 119 us -> 8.91 us
  loops' own time: 105 us -> 0 us
  Pallas kernels: 0 us -> 55.3 us
  local copies, waits for them, and re-layouts: 40.4 us -> 1.55 us
  waiting for transfers between devices: 111 us -> 76.9 us
  blocking collectives: 0 us -> 25 us
  starting transfers between devices: 40.4 us -> 17.6 us
    dot_general x263 -> x0, matrix products: 270 us -> none  [the longest x128 116 us: step(): rest = grow - jnp.dot(column, factor, precision=lax.Precision.HIGHEST)]
    another operation x2 -> x0, loops' own time: 105 us -> none  [the longest x1 100 us: upper_factor(): return lax.fori_loop(0, order, step, jnp.zeros_like(gram_total))]
    reduce_sum x130 -> x5, other arithmetic: 89.7 us -> 4.56 us  [the longest x1 2.91 us: body(): filled = jnp.sum((slot_in > 0).astype(jnp.int32))]
    pallas_call x0 -> x6, Pallas kernels: none -> 55.3 us  [the longest x2 17.9 us: apply_inverse(): pl.pallas_call(functools.partial(apply_kernel, lo), grid_spec=pltpu.Prefe...]
    all_to_all x0 -> x1, blocking collectives: none -> 25 us  [exchange(): lax.all_to_all(payload, AXES, split_axis=0, concat_axis=0, tiled=True)]
    add x264 -> x1, other arithmetic: 23.9 us -> 0.83 us  [body(): code = block_owner * 128 + block_slot]
    all_to_all x2 -> x3, waiting for transfers between devices: 97.6 us -> 76.9 us  [exchange(): lax.all_to_all(payload, AXES, split_axis=0, concat_axis=0, tiled=True)]
    ppermute x7 -> x0, starting transfers between devices: 15.4 us -> none  [swapped(): lax.ppermute(value, axis, [(i, i ^ 1 << stride) for i in range(lax.axis_s...]
  transfers between devices with their start and end apart: 9 -> 3, of which waited for: 7 -> 3; matrix products, arithmetic and copies ran while one was open for 55% -> 4% of each run, Pallas kernels for 0% -> 19%
where the time goes in v1:
time: 187 us; the launch traced here: 186 us
  waiting for transfers between devices  76.9 us (41%)
  Pallas kernels  55.3 us (30%)
  blocking collectives  25 us (13%)
  starting transfers between devices  17.6 us (9%)
  other arithmetic  8.91 us (5%)
    all_to_all x3, waiting for transfers between devices, exchange(): lax.all_to_all(payload, AXES, split_axis=0, concat_axis=0, tiled=True)  76.9 us
    all_to_all x1, blocking collectives, exchange(): lax.all_to_all(payload, AXES, split_axis=0, concat_axis=0, tiled=True)  25 us
    pallas_call x2, Pallas kernels, apply_inverse(): pl.pallas_call(functools.partial(apply_kernel, lo), grid_spec=pltpu.Prefe...  17.9 us
    all_to_all x3, starting transfers between devices, exchange(): lax.all_to_all(payload, AXES, split_axis=0, concat_axis=0, tiled=True)  17.6 us
    pallas_call x1, Pallas kernels, finish(): pl.pallas_call(functools.partial(finish_kernel, float(row_total)), out_sh...  16.7 us
    pallas_call x1, Pallas kernels, gram_pair(): pl.pallas_call(gram_kernel, grid=(count // GRAM_STEP,), in_specs=[pl.Bloc...  11.6 us
    pallas_call x2, Pallas kernels, pack(): pl.pallas_call(functools.partial(pack_kernel, height, lo), grid_spec=pltp...  9.11 us
  transfers between devices with their start and end apart: 3, of which 3 were waited for; matrix products, arithmetic and copies ran while one was open for 4% of the time, Pallas kernels for 19%

profile of v1, /device:TPU:1, one launch (start us, length us, event | category | flops | bytes accessed | tf_op | source)
XLA Modules:
  0.0 186.0 jit_solution(17662613163315144454)
XLA Ops:
  0.6 0.8 multiply_add_fusion
  1.5 1.3 select_reduce_fusion
  2.8 0.0 copy-start.1
  2.8 0.1 select_reduce_fusion.2
  2.9 0.7 broadcast_in_dim.57.note_ref
  3.6 11.6 %gram.1 = f32[128,8,128]{2,1,0:T(8,128)} custom-call(f32[128,128]{1,0:T(8,128)} %broadcast_in_dim.57.note_ref, f32[96,128,128]{2,1,0:T(8,128)} %early_ref.1, f32[96,128,128]{2,1,0:T(8,128)} %late_ref.5), custom_call_target="tpu_custom_call" | custom-call | flops 2415919104 | bytes 8388608 | tf_op jit(solution)/shard_map/gram/pallas_call | solution.py:106
  15.2 0.0 copy-done.1
  15.2 25.0 %all_to_all.20 = f32[128,8,128]{2,1,0:T(8,128)S(1)} all-to-all(f32[128,8,128]{2,1,0:T(8,128)} %gram.1), channel_id=1, replica_groups=mesh['rows'=64,'grp'=2] {'rows','grp'}, dimensions={0} | all-to-all | bytes 1048576 | tf_op jit(solution)/shard_map/all_to_all | solution.py:254
  40.2 0.1 reduce_sum.49
  40.3 0.8 broadcast_in_dim.60
  41.2 4.6 %all-to-all-start.1 = ((f32[128,8,128]{2,1,0:T(8,128)}), f32[128,8,128]{2,1,0:T(8,128)S(1)}, u32[]{:S(2)}, u32[]{:S(2)}) async-start(f32[128,8,128]{2,1,0:T(8,128)} %broadcast_in_dim.60), calls=%async_computation.1 | async-start | bytes 1048576 | tf_op jit(solution)/shard_map/all_to_all | solution.py:254
  45.8 4.6 %pack.3 = f32[128,64,128]{2,1,0:T(8,128)} custom-call(s32[96]{0:T(128)} %copy-done.1, f32[96,128,128]{2,1,0:T(8,128)} %late_ref.5), custom_call_target="tpu_custom_call" | custom-call | flops 100000000 | bytes 8388608 | tf_op jit(solution)/shard_map/pack/pallas_call | solution.py:52
  50.4 9.1 %all-to-all-done.1.stats_ref = f32[128,8,128]{2,1,0:T(8,128)S(1)} async-done(((f32[128,8,128]{2,1,0:T(8,128)}), f32[128,8,128]{2,1,0:T(8,128)S(1)}, u32[]{:S(2)}, u32[]{:S(2)}) %all-to-all-start.1) | async-done | bytes 524320 | tf_op jit(solution)/shard_map/all_to_all | solution.py:254
  59.5 0.0 copy-start
  59.5 5.8 %all-to-all-start.3 = ((f32[128,64,128]{2,1,0:T(8,128)}), f32[128,64,128]{2,1,0:T(8,128)}, u32[]{:S(2)}, u32[]{:S(2)}) async-start(f32[128,64,128]{2,1,0:T(8,128)} %pack.3), calls=%async_computation.3 | async-start | bytes 8388608 | tf_op jit(solution)/shard_map/all_to_all | solution.py:254
  65.2 4.5 %pack.2 = f32[128,64,128]{2,1,0:T(8,128)} custom-call(s32[96]{0:T(128)} %copy-done.1, f32[96,128,128]{2,1,0:T(8,128)} %late_ref.5), custom_call_target="tpu_custom_call" | custom-call | flops 100000000 | bytes 8388608 | tf_op jit(solution)/shard_map/pack/pallas_call | solution.py:52
  69.8 0.0 copy-done
  69.8 47.8 %all-to-all-done.3.arrived_ref = f32[128,64,128]{2,1,0:T(8,128)} async-done(((f32[128,64,128]{2,1,0:T(8,128)}), f32[128,64,128]{2,1,0:T(8,128)}, u32[]{:S(2)}, u32[]{:S(2)}) %all-to-all-start.3) | async-done | bytes 4194336 | tf_op jit(solution)/shard_map/all_to_all | solution.py:254
  117.6 7.2 %all-to-all-start.2 = ((f32[128,64,128]{2,1,0:T(8,128)}), f32[128,64,128]{2,1,0:T(8,128)}, u32[]{:S(2)}, u32[]{:S(2)}) async-start(f32[128,64,128]{2,1,0:T(8,128)} %pack.2), calls=%async_computation.2 | async-start | bytes 8388608 | tf_op jit(solution)/shard_map/all_to_all | solution.py:254
  124.9 2.4 %compare_reduce_fusion = pred[128]{0:T(512)(128)(4,1)S(1)} fusion(f32[128,8,128]{2,1,0:T(8,128)S(1)} %all_to_all.20), kind=kLoop, calls=%fused_computation.3 | loop fusion | flops 256 | bytes 640 | tf_op jit(solution)/shard_map/eq | solution.py:281
  127.2 0.1 select_reduce_fusion.1
  127.3 2.9 %fusion = (s32[]{:T(128)}, s32[128]{0:T(128)S(1)}) fusion(f32[128,8,128]{2,1,0:T(8,128)S(1)} %all_to_all.20), kind=kLoop, calls=%fused_computation.4 | loop fusion | flops 639 | bytes 1028 | tf_op jit(solution)/shard_map/reduce_sum | solution.py:282
  130.2 1.1 add_select_fusion.place_ref
  131.4 16.7 %finish.1 = (bf16[256,256]{1,0:T(8,128)(2,1)}, f32[128,128]{1,0:T(8,128)}) custom-call(f32[128,8,128]{2,1,0:T(8,128)} %copy-done), custom_call_target="tpu_custom_call" | custom-call | flops 1000000000 | bytes 524288 | tf_op jit(solution)/shard_map/finish/pallas_call | solution.py:156
  148.1 9.0 %apply.2.rest_0_ = f32[128,128,128]{2,1,0:T(8,128)} custom-call(s32[128]{0:T(128)} %add_select_fusion.place_ref, bf16[256,256]{1,0:T(8,128)(2,1)} %get-tuple-element.4.weight_ref, f32[128,64,128]{2,1,0:T(8,128)} %all-to-all-done.3.arrived_ref), custom_call_target="tpu_custom_call" | custom-call | flops 1073741824 | bytes 8388608 | tf_op jit(solution)/shard_map/apply/pallas_call | solution.py:230
  157.1 20.0 %all-to-all-done.2.arrived_ref = f32[128,64,128]{2,1,0:T(8,128)} async-done(((f32[128,64,128]{2,1,0:T(8,128)}), f32[128,64,128]{2,1,0:T(8,128)}, u32[]{:S(2)}, u32[]{:S(2)}) %all-to-all-start.2) | async-done | bytes 4194336 | tf_op jit(solution)/shard_map/all_to_all | solution.py:254
  177.1 8.9 %apply.3 = f32[128,128,128]{2,1,0:T(8,128)} custom-call(s32[128]{0:T(128)} %add_select_fusion.place_ref, bf16[256,256]{1,0:T(8,128)(2,1)} %get-tuple-element.4.weight_ref, f32[128,64,128]{2,1,0:T(8,128)} %all-to-all-done.2.arrived_ref, f32[128,128,128]{2,1,0:T(8,128)} %apply.2.rest_0_), custom_call_target="tpu_custom_call", output_to_operand_aliasing={{}: (3, {})} | custom-call | flops 1073741824 | bytes 8388608 | tf_op jit(solution)/shard_map/apply/pallas_call | solution.py:230
  (2 shorter events, 0.0 us)
Async XLA Ops:
  2.8 12.4 %copy-start.1 = (s32[96]{0:T(128)}, s32[96]{0:T(128)S(1)}, u32[]{:S(2)}) copy-start(s32[96]{0:T(128)S(1)} %get-tuple-element.8.dest_ref) | copy-start | bytes 1156
  41.2 18.3 %all-to-all-start.1 = ((f32[128,8,128]{2,1,0:T(8,128)}), f32[128,8,128]{2,1,0:T(8,128)S(1)}, u32[]{:S(2)}, u32[]{:S(2)}) async-start(f32[128,8,128]{2,1,0:T(8,128)} %broadcast_in_dim.60), calls=%async_computation.1 | async-start | bytes 1048576 | tf_op jit(solution)/shard_map/all_to_all | solution.py:254
  59.5 10.3 %copy-start = (f32[128,8,128]{2,1,0:T(8,128)}, f32[128,8,128]{2,1,0:T(8,128)S(1)}, u32[]{:S(2)}) copy-start(f32[128,8,128]{2,1,0:T(8,128)S(1)} %all-to-all-done.1.stats_ref) | copy-start | bytes 1572868
  59.5 58.1 %all-to-all-start.3 = ((f32[128,64,128]{2,1,0:T(8,128)}), f32[128,64,128]{2,1,0:T(8,128)}, u32[]{:S(2)}, u32[]{:S(2)}) async-start(f32[128,64,128]{2,1,0:T(8,128)} %pack.3), calls=%async_computation.3 | async-start | bytes 8388608 | tf_op jit(solution)/shard_map/all_to_all | solution.py:254
  117.6 59.5 %all-to-all-start.2 = ((f32[128,64,128]{2,1,0:T(8,128)}), f32[128,64,128]{2,1,0:T(8,128)}, u32[]{:S(2)}, u32[]{:S(2)}) async-start(f32[128,64,128]{2,1,0:T(8,128)} %pack.2), calls=%async_computation.2 | async-start | bytes 8388608 | tf_op jit(solution)/shard_map/all_to_all | solution.py:254

commit v2 on v1

v2 whole, which is shorter than its diff:
```python
import functools

import jax
import jax.numpy as jnp
from jax import lax
from jax.experimental import pallas as pl
from jax.experimental.pallas import tpu as pltpu
from jax.sharding import PartitionSpec as P

AXES = ("rows", "grp")
GRAM_CHUNKS = (16, 32, 48)
PACK_CHUNKS = 4
APPLY_STEP = 16
NOTE_ROWS = 4
CAP = 128


def split_pair(x):
    hi = x.astype(jnp.bfloat16)
    lo = (x - hi.astype(jnp.float32)).astype(jnp.bfloat16)
    return hi, lo


def contract_rows(a, b):
    return lax.dot_general(
        a, b, (((0,), (0,)), ((), ())), preferred_element_type=jnp.float32
    )


def pack_kernel(dest_ref, late_ref, out_ref, buf, sem_in, sem_out):
    count = late_ref.shape[0]
    size = count // PACK_CHUNKS

    def load(t):
        part = pl.ds(t * size, size)
        return pltpu.make_async_copy(late_ref.at[part], buf.at[part], sem_in.at[t])

    for t in range(PACK_CHUNKS):
        load(t).start()
    for t in range(PACK_CHUNKS):
        load(t).wait()

        def send(i, carry):
            pltpu.make_async_copy(buf.at[i], out_ref.at[dest_ref[i]], sem_out).start()
            return carry

        lax.fori_loop(t * size, t * size + size, send, 0, unroll=8)
    pltpu.make_async_copy(buf, out_ref.at[pl.ds(0, count)], sem_out).wait()


def pack(late, dest, members):
    count, block, width = late.shape
    return pl.pallas_call(
        pack_kernel,
        grid_spec=pltpu.PrefetchScalarGridSpec(
            num_scalar_prefetch=1,
            grid=(1,),
            in_specs=[pl.BlockSpec(memory_space=pl.ANY)],
            out_specs=pl.BlockSpec(memory_space=pl.ANY),
            scratch_shapes=[
                pltpu.VMEM((count, block, width), jnp.float32),
                pltpu.SemaphoreType.DMA((PACK_CHUNKS,)),
                pltpu.SemaphoreType.DMA,
            ],
        ),
        out_shape=jax.ShapeDtypeStruct((members, block, width), jnp.float32),
        cost_estimate=pl.CostEstimate(flops=100000000, bytes_accessed=1 << 23, transcendentals=0),
        name="pack",
    )(dest, late)


def gram_kernel(early_ref, late_ref, out_ref, early_buf, late_buf, sem_early, sem_late):
    width = early_ref.shape[2]
    parts = []
    lo = 0
    for k, size in enumerate(GRAM_CHUNKS):
        part = pl.ds(lo, size)
        one = pltpu.make_async_copy(early_ref.at[part], early_buf.at[part], sem_early.at[k])
        two = pltpu.make_async_copy(late_ref.at[part], late_buf.at[part], sem_late.at[k])
        one.start()
        two.start()
        parts.append((part, one, two))
        lo += size
    gram_wide = cross_wide = None
    for part, one, two in parts:
        one.wait()
        two.wait()
        ehi, elo = split_pair(early_buf[part].reshape((-1, width)))
        lhi, llo = split_pair(late_buf[part].reshape((-1, width)))
        pair = jnp.concatenate([ehi, elo], axis=1)
        gram_part = contract_rows(ehi, pair)
        cross_part = contract_rows(pair, jnp.concatenate([lhi, llo], axis=1))
        gram_wide = gram_part if gram_wide is None else gram_wide + gram_part
        cross_wide = cross_part if cross_wide is None else cross_wide + cross_part
    mixed = gram_wide[:, width:]
    out_ref[:, 0, :] = gram_wide[:, 0:width] + (mixed + mixed.T)
    out_ref[:, 1, :] = cross_wide[0:width, 0:width] + (
        cross_wide[0:width, width:] + cross_wide[width:, 0:width]
    )


def gram_pair(early, late):
    count, block, width = early.shape
    steps = len(GRAM_CHUNKS)
    anywhere = pl.BlockSpec(memory_space=pl.ANY)
    return pl.pallas_call(
        gram_kernel,
        in_specs=[anywhere, anywhere],
        out_specs=pl.BlockSpec(memory_space=pltpu.VMEM),
        out_shape=jax.ShapeDtypeStruct((width, 2, width), jnp.float32),
        scratch_shapes=[
            pltpu.VMEM((count, block, width), jnp.float32),
            pltpu.VMEM((count, block, width), jnp.float32),
            pltpu.SemaphoreType.DMA((steps,)),
            pltpu.SemaphoreType.DMA((steps,)),
        ],
        cost_estimate=pl.CostEstimate(
            flops=12 * count * block * width * width, bytes_accessed=1 << 23, transcendentals=0
        ),
        name="gram",
    )(early, late)


def mix_kernel(partial_ref, note_ref, out_ref):
    members, _, width = partial_ref.shape
    gram_row = jnp.sum(partial_ref[:, 0, :], axis=0, keepdims=True)
    cross_row = jnp.sum(partial_ref[:, 1, :], axis=0, keepdims=True)
    out_ref[:, 0, :] = jnp.broadcast_to(gram_row, (members, width))
    out_ref[:, 1, :] = jnp.broadcast_to(cross_row, (members, width))
    out_ref[:, 2, :] = note_ref[...]
    out_ref[:, 3, :] = jnp.zeros((members, width), jnp.float32)


def mix(partial, note):
    members, _, width = partial.shape
    return pl.pallas_call(
        mix_kernel,
        out_shape=jax.ShapeDtypeStruct((members, NOTE_ROWS, width), jnp.float32),
        cost_estimate=pl.CostEstimate(flops=1000000, bytes_accessed=1 << 19, transcendentals=0),
        compiler_params=pltpu.CompilerParams(vmem_limit_bytes=4 << 20),
        name="mix",
    )(partial, note)


def dot3(a, b):
    return jnp.dot(a, b, precision=lax.Precision.HIGHEST, preferred_element_type=jnp.float32)


def finish_kernel(row_total, stats_ref, weight_ref, operator_ref, work):
    order = stats_ref.shape[0]
    row_id = lax.broadcasted_iota(jnp.int32, (order, 1), 0)
    lane = lax.broadcasted_iota(jnp.int32, (1, 2 * order), 1)
    lane_half = lax.broadcasted_iota(jnp.int32, (1, order), 1)
    work[:, 0:order] = stats_ref[:, 0, :] / row_total
    work[:, order:] = (row_id == lane_half).astype(jnp.float32)

    def step(j, carry):
        row = work[pl.ds(j, 1), :]
        inv = lax.rsqrt(jnp.sum(jnp.where(lane == j, row, 0.0), axis=1, keepdims=True))
        scaled = row * inv
        table = work[...]
        column = jnp.sum(
            jnp.where(lane_half == j, table[:, 0:order], 0.0), axis=1, keepdims=True
        )
        down = jnp.where(row_id > j, column * inv, 0.0)
        work[...] = jnp.where(row_id == j, scaled, table - down * scaled)
        return carry

    lax.fori_loop(0, order, step, 0)
    inverse_t = work[:, order:]
    inverse = inverse_t.T
    cross = stats_ref[:, 1, :] / row_total
    operator_ref[...] = dot3(inverse_t, dot3(cross, inverse))
    whi, wlo = split_pair(inverse)
    weight_ref[0:order, 0:order] = whi
    weight_ref[0:order, order:] = wlo
    weight_ref[order:, 0:order] = whi
    weight_ref[order:, order:] = wlo


def finish(stats, row_total):
    order = stats.shape[0]
    return pl.pallas_call(
        functools.partial(finish_kernel, float(row_total)),
        out_shape=(
            jax.ShapeDtypeStruct((2 * order, 2 * order), jnp.bfloat16),
            jax.ShapeDtypeStruct((order, order), jnp.float32),
        ),
        scratch_shapes=[pltpu.VMEM((order, 2 * order), jnp.float32)],
        cost_estimate=pl.CostEstimate(flops=1000000000, bytes_accessed=1 << 19, transcendentals=0),
        compiler_params=pltpu.CompilerParams(vmem_limit_bytes=4 << 20),
        name="finish",
    )(stats)


def apply_kernel(place_ref, weight_ref, arrived_ref, out_ref, buf_in, buf_out, sem_in, sem_out):
    count, block, width = arrived_ref.shape
    steps = count // APPLY_STEP

    def fetch(t):
        part = pl.ds(t * APPLY_STEP, APPLY_STEP)
        return pltpu.make_async_copy(arrived_ref.at[part], buf_in.at[part], sem_in.at[t])

    for t in range(steps):
        fetch(t).start()

    def step(t, carry):
        part = pl.ds(t * APPLY_STEP, APPLY_STEP)
        fetch(t).wait()
        hi, lo = split_pair(buf_in[part].reshape((APPLY_STEP * block, width)))
        wide = jnp.dot(
            jnp.concatenate([hi, lo], axis=1),
            weight_ref[...],
            preferred_element_type=jnp.float32,
        )
        solved = wide[:, 0:width] + wide[:, width:]
        buf_out[part] = solved.reshape((APPLY_STEP, block, width))
        for i in range(APPLY_STEP):
            row = t * APPLY_STEP + i
            code = place_ref[row]

            @pl.when(code >= count)
            def _():
                buf_out[row] = jnp.zeros((block, width), jnp.float32)

            pltpu.make_async_copy(
                buf_out.at[row], out_ref.at[lax.rem(code, count)], sem_out
            ).start()
        return carry

    lax.fori_loop(0, steps, step, 0)
    pltpu.make_async_copy(buf_out, out_ref, sem_out).wait()


def apply_inverse(place, weight, arrived):
    count, block, width = arrived.shape
    anywhere = pl.BlockSpec(memory_space=pl.ANY)
    return pl.pallas_call(
        apply_kernel,
        grid_spec=pltpu.PrefetchScalarGridSpec(
            num_scalar_prefetch=1,
            grid=(1,),
            in_specs=[pl.BlockSpec(memory_space=pltpu.VMEM), anywhere],
            out_specs=anywhere,
            scratch_shapes=[
                pltpu.VMEM((count, block, width), jnp.float32),
                pltpu.VMEM((count, block, width), jnp.float32),
                pltpu.SemaphoreType.DMA((count // APPLY_STEP,)),
                pltpu.SemaphoreType.DMA,
            ],
        ),
        out_shape=jax.ShapeDtypeStruct((count, block, width), jnp.float32),
        cost_estimate=pl.CostEstimate(
            flops=8 * count * block * width * width, bytes_accessed=1 << 23, transcendentals=0
        ),
        compiler_params=pltpu.CompilerParams(vmem_limit_bytes=24 << 20),
        name="apply",
    )(place, weight, arrived)


def exchange(payload):
    return lax.all_to_all(payload, AXES, split_axis=0, concat_axis=0, tiled=True)


def body(snap_early, snap_late, block_ids, block_owner, block_slot):
    members = lax.axis_size(AXES)
    count, block, width = snap_late.shape
    row_total = count * block * members
    outgoing = gram_pair(snap_early, snap_late)
    block_ids, outgoing = lax.optimization_barrier((block_ids, outgoing))
    partial = exchange(outgoing)
    labels = jnp.arange(block_owner.shape[0], dtype=jnp.int32)
    code = block_owner * CAP + block_slot
    hits = block_ids[:, None] == labels[None, :]
    code_here = jnp.sum(jnp.where(hits, code[None, :], 0), axis=1)
    dest = code_here // CAP
    slot_here = code_here % CAP
    target = jnp.arange(members, dtype=jnp.int32)
    note = jnp.sum(
        jnp.where(dest[None, :] == target[:, None], slot_here[None, :] + 1, 0), axis=1
    )
    note = jnp.broadcast_to(note.astype(jnp.float32)[:, None], (members, width))
    payload = pack(snap_late, dest, members)
    stats = exchange(mix(partial, note))
    payload, _ = lax.optimization_barrier((payload, stats))
    arrived = exchange(payload)
    weight, operator = finish(stats, row_total)
    slot_in = stats[:, 2, 0].astype(jnp.int32)
    empty = slot_in == 0
    filled = jnp.sum((slot_in > 0).astype(jnp.int32))
    earlier = jnp.sum(
        jnp.where(empty[None, :] & (target[None, :] < target[:, None]), 1, 0), axis=1
    )
    place = jnp.where(empty, filled + earlier + CAP, slot_in - 1)
    modes = apply_inverse(place, weight, arrived)
    return (modes, operator)


def solution(mesh):
    placed = (
        P(AXES, None, None),
        P(AXES, None, None),
        P(AXES),
        P(),
        P(),
    )
    return jax.shard_map(
        body,
        mesh=mesh,
        in_specs=placed,
        out_specs=(P(AXES, None, None), P()),
        check_vma=False,
    )
```

time: 187 us -> 163 us (0.87)
  blocking collectives: 25 us -> 0 us
  Pallas kernels: 55.3 us -> 37 us
  waiting for transfers between devices: 76.9 us -> 94.1 us
  starting transfers between devices: 17.6 us -> 21.5 us
  other arithmetic: 8.91 us -> 6.88 us
    all_to_all x1 -> x0, blocking collectives: 25 us -> none  [exchange(): lax.all_to_all(payload, AXES, split_axis=0, concat_axis=0, tiled=True)]
    pallas_call x5 -> x4, Pallas kernels: 38.6 us -> 21.3 us  [the longest x1 7.41 us: apply_inverse(): pl.pallas_call(apply_kernel, grid_spec=pltpu.PrefetchScalarGridSpec(num_s...]
    all_to_all x3, waiting for transfers between devices: 76.9 us -> 94.1 us  [exchange(): lax.all_to_all(payload, AXES, split_axis=0, concat_axis=0, tiled=True)]
    all_to_all x3, starting transfers between devices: 17.6 us -> 21.5 us  [exchange(): lax.all_to_all(payload, AXES, split_axis=0, concat_axis=0, tiled=True)]
  transfers between devices with their start and end apart: 3 -> 3, of which waited for: 3 -> 3; matrix products, arithmetic and copies ran while one was open for 4% -> 4% of each run, Pallas kernels for 19% -> 13%
where the time goes in v2:
time: 163 us; the launch traced here: 160 us
  waiting for transfers between devices  94.1 us (58%)
  Pallas kernels  37 us (23%)
  starting transfers between devices  21.5 us (13%)
  other arithmetic  6.88 us (4%)
    all_to_all x3, waiting for transfers between devices, exchange(): lax.all_to_all(payload, AXES, split_axis=0, concat_axis=0, tiled=True)  94.1 us
    all_to_all x3, starting transfers between devices, exchange(): lax.all_to_all(payload, AXES, split_axis=0, concat_axis=0, tiled=True)  21.5 us
    pallas_call x1, Pallas kernels, finish(): pl.pallas_call(functools.partial(finish_kernel, float(row_total)), out_sh...  15.7 us
    pallas_call x1, Pallas kernels, apply_inverse(): pl.pallas_call(apply_kernel, grid_spec=pltpu.PrefetchScalarGridSpec(num_s...  7.41 us
    pallas_call x1, Pallas kernels, gram_pair(): pl.pallas_call(gram_kernel, in_specs=[anywhere, anywhere], out_specs=pl.B...  7.25 us
    pallas_call x1, Pallas kernels, pack(): pl.pallas_call(pack_kernel, grid_spec=pltpu.PrefetchScalarGridSpec(num_sc...  5.76 us
  transfers between devices with their start and end apart: 3, of which 3 were waited for; matrix products, arithmetic and copies ran while one was open for 4% of the time, Pallas kernels for 13%

profile of v2, /device:TPU:1, one launch (start us, length us, event | category | flops | bytes accessed | tf_op | source)
XLA Modules:
  0.0 160.3 jit_solution(366296403647537627)
XLA Ops:
  0.6 0.0 copy-start.2
  0.6 0.0 copy-start
  0.7 0.0 copy-start.1
  0.7 7.2 %gram.1 = f32[128,2,128]{2,1,0:T(2,128)} custom-call(f32[96,128,128]{2,1,0:T(8,128)} %early_ref.1, f32[96,128,128]{2,1,0:T(8,128)} %late_ref.3), custom_call_target="tpu_custom_call" | custom-call | flops 2415919104 | bytes 8388608 | tf_op jit(solution)/shard_map/gram/pallas_call | solution.py:106
  7.9 11.5 %all-to-all-start = ((f32[128,2,128]{2,1,0:T(2,128)}), f32[128,2,128]{2,1,0:T(2,128)S(1)}, u32[]{:S(2)}, u32[]{:S(2)}) async-start(f32[128,2,128]{2,1,0:T(2,128)} %gram.1), calls=%async_computation | async-start | bytes 262144 | tf_op jit(solution)/shard_map/all_to_all | solution.py:262
  19.4 0.0 copy-done
  19.4 0.0 copy-done.1
  19.5 0.0 copy-done.2
  19.5 0.8 select_reduce_fusion
  20.3 0.0 copy-start.3
  20.3 0.1 select_reduce_fusion.2
  20.4 8.8 %all-to-all-done.partial_ref = f32[128,2,128]{2,1,0:T(2,128)S(1)} async-done(((f32[128,2,128]{2,1,0:T(2,128)}), f32[128,2,128]{2,1,0:T(2,128)S(1)}, u32[]{:S(2)}, u32[]{:S(2)}) %all-to-all-start) | async-done | bytes 131104 | tf_op jit(solution)/shard_map/all_to_all | solution.py:262
  29.2 0.1 broadcast_in_dim.51.note_ref
  29.3 0.9 mix.1
  30.2 4.3 %all-to-all-start.1 = ((f32[128,4,128]{2,1,0:T(4,128)}), f32[128,4,128]{2,1,0:T(4,128)S(1)}, u32[]{:S(2)}, u32[]{:S(2)}) async-start(f32[128,4,128]{2,1,0:T(4,128)} %mix.1), calls=%async_computation.1 | async-start | bytes 524288 | tf_op jit(solution)/shard_map/all_to_all | solution.py:262
  34.5 0.0 copy-done.3
  34.5 5.8 %pack.1 = f32[128,128,128]{2,1,0:T(8,128)} custom-call(s32[96]{0:T(128)} %copy-done.3, f32[96,128,128]{2,1,0:T(8,128)} %late_ref.3), custom_call_target="tpu_custom_call" | custom-call | flops 100000000 | bytes 8388608 | tf_op jit(solution)/shard_map/pack/pallas_call | solution.py:53
  40.3 5.2 %all-to-all-done.1.stats_ref = f32[128,4,128]{2,1,0:T(4,128)S(1)} async-done(((f32[128,4,128]{2,1,0:T(4,128)}), f32[128,4,128]{2,1,0:T(4,128)S(1)}, u32[]{:S(2)}, u32[]{:S(2)}) %all-to-all-start.1) | async-done | bytes 262176 | tf_op jit(solution)/shard_map/all_to_all | solution.py:262
  45.5 5.7 %all-to-all-start.2 = ((f32[128,128,128]{2,1,0:T(8,128)}), f32[128,128,128]{2,1,0:T(8,128)}, u32[]{:S(2)}, u32[]{:S(2)}) async-start(f32[128,128,128]{2,1,0:T(8,128)} %pack.1), calls=%async_computation.2 | async-start | bytes 16777216 | tf_op jit(solution)/shard_map/all_to_all | solution.py:262
  51.3 15.7 %finish.1 = (bf16[256,256]{1,0:T(8,128)(2,1)S(1)}, f32[128,128]{1,0:T(8,128)}) custom-call(f32[128,4,128]{2,1,0:T(4,128)S(1)} %all-to-all-done.1.stats_ref), custom_call_target="tpu_custom_call" | custom-call | flops 1000000000 | bytes 524288 | tf_op jit(solution)/shard_map/finish/pallas_call | solution.py:183
  66.9 2.4 %compare_reduce_fusion = pred[128]{0:T(512)(128)(4,1)S(1)} fusion(f32[128,4,128]{2,1,0:T(4,128)S(1)} %all-to-all-done.1.stats_ref), kind=kLoop, calls=%fused_computation.3 | loop fusion | flops 256 | bytes 640 | tf_op jit(solution)/shard_map/eq | solution.py:289
  69.3 0.1 select_reduce_fusion.1
  69.4 2.9 %fusion = (s32[]{:T(128)}, s32[128]{0:T(128)S(1)}) fusion(f32[128,4,128]{2,1,0:T(4,128)S(1)} %all-to-all-done.1.stats_ref), kind=kLoop, calls=%fused_computation.4 | loop fusion | flops 639 | bytes 1028 | tf_op jit(solution)/shard_map/reduce_sum | solution.py:290
  72.3 0.6 add_select_fusion.place_ref
  72.9 80.0 %all-to-all-done.2.arrived_ref = f32[128,128,128]{2,1,0:T(8,128)} async-done(((f32[128,128,128]{2,1,0:T(8,128)}), f32[128,128,128]{2,1,0:T(8,128)}, u32[]{:S(2)}, u32[]{:S(2)}) %all-to-all-start.2) | async-done | bytes 8388640 | tf_op jit(solution)/shard_map/all_to_all | solution.py:262
  152.9 7.4 %apply.1 = f32[128,128,128]{2,1,0:T(8,128)} custom-call(s32[128]{0:T(128)S(1)} %add_select_fusion.place_ref, bf16[256,256]{1,0:T(8,128)(2,1)S(1)} %get-tuple-element.9.weight_ref, f32[128,128,128]{2,1,0:T(8,128)} %all-to-all-done.2.arrived_ref), custom_call_target="tpu_custom_call" | custom-call | flops 2147483648 | bytes 8388608 | tf_op jit(solution)/shard_map/apply/pallas_call | solution.py:238
  (3 shorter events, 0.0 us)
Async XLA Ops:
  0.6 18.8 %copy-start.2 = (s32[96]{0:T(128)S(1)}, s32[96]{0:T(128)}, u32[]{:S(2)}) copy-start(s32[96]{0:T(128)} %param.7) | copy-start | bytes 1156
  0.6 18.8 %copy-start = (s32[12288]{0:T(1024)S(1)}, s32[12288]{0:T(1024)}, u32[]{:S(2)}) copy-start(s32[12288]{0:T(1024)} %param.9) | copy-start | bytes 147460
  0.7 18.8 %copy-start.1 = (s32[12288]{0:T(1024)S(1)}, s32[12288]{0:T(1024)}, u32[]{:S(2)}) copy-start(s32[12288]{0:T(1024)} %param.8) | copy-start | bytes 147460
  7.9 21.3 %all-to-all-start = ((f32[128,2,128]{2,1,0:T(2,128)}), f32[128,2,128]{2,1,0:T(2,128)S(1)}, u32[]{:S(2)}, u32[]{:S(2)}) async-start(f32[128,2,128]{2,1,0:T(2,128)} %gram.1), calls=%async_computation | async-start | bytes 262144 | tf_op jit(solution)/shard_map/all_to_all | solution.py:262
  20.3 14.2 %copy-start.3 = (s32[96]{0:T(128)}, s32[96]{0:T(128)S(1)}, u32[]{:S(2)}) copy-start(s32[96]{0:T(128)S(1)} %get-tuple-element.14.dest_ref) | copy-start | bytes 1156
  30.2 15.3 %all-to-all-start.1 = ((f32[128,4,128]{2,1,0:T(4,128)}), f32[128,4,128]{2,1,0:T(4,128)S(1)}, u32[]{:S(2)}, u32[]{:S(2)}) async-start(f32[128,4,128]{2,1,0:T(4,128)} %mix.1), calls=%async_computation.1 | async-start | bytes 524288 | tf_op jit(solution)/shard_map/all_to_all | solution.py:262
  45.5 107.4 %all-to-all-start.2 = ((f32[128,128,128]{2,1,0:T(8,128)}), f32[128,128,128]{2,1,0:T(8,128)}, u32[]{:S(2)}, u32[]{:S(2)}) async-start(f32[128,128,128]{2,1,0:T(8,128)} %pack.1), calls=%async_computation.2 | async-start | bytes 16777216 | tf_op jit(solution)/shard_map/all_to_all | solution.py:262

commit v3 on v2

--- a/solution.py
+++ b/solution.py
@@ -10,8 +10,8 @@
 AXES = ("rows", "grp")
 GRAM_CHUNKS = (16, 32, 48)
 PACK_CHUNKS = 4
-APPLY_STEP = 16
-NOTE_ROWS = 4
+NOTE_ROWS = 8
+LAST_ROWS = 16
 CAP = 128
 
 
@@ -27,9 +27,11 @@
     )
 
 
-def pack_kernel(dest_ref, late_ref, out_ref, buf, sem_in, sem_out):
-    count = late_ref.shape[0]
+def pack_kernel(dest_ref, late_ref, first_ref, last_ref, buf, sem_in, sem_out, sem_last):
+    count, block, _ = late_ref.shape
     size = count // PACK_CHUNKS
+    last = last_ref.shape[1]
+    first = block - last
 
     def load(t):
         part = pl.ds(t * size, size)
@@ -41,29 +43,45 @@
         load(t).wait()
 
         def send(i, carry):
-            pltpu.make_async_copy(buf.at[i], out_ref.at[dest_ref[i]], sem_out).start()
+            row = dest_ref[i]
+            pltpu.make_async_copy(
+                buf.at[i, pl.ds(0, first)], first_ref.at[row, pl.ds(0, first)], sem_out
+            ).start()
+            pltpu.make_async_copy(
+                buf.at[i, pl.ds(first, last)], last_ref.at[row], sem_last
+            ).start()
             return carry
 
         lax.fori_loop(t * size, t * size + size, send, 0, unroll=8)
-    pltpu.make_async_copy(buf, out_ref.at[pl.ds(0, count)], sem_out).wait()
+    every = pl.ds(0, count)
+    pltpu.make_async_copy(
+        buf.at[:, pl.ds(0, first)], first_ref.at[every, pl.ds(0, first)], sem_out
+    ).wait()
+    pltpu.make_async_copy(buf.at[:, pl.ds(first, last)], last_ref.at[every], sem_last).wait()
 
 
 def pack(late, dest, members):
     count, block, width = late.shape
+    anywhere = pl.BlockSpec(memory_space=pl.ANY)
+    first = block - LAST_ROWS
     return pl.pallas_call(
         pack_kernel,
         grid_spec=pltpu.PrefetchScalarGridSpec(
             num_scalar_prefetch=1,
             grid=(1,),
-            in_specs=[pl.BlockSpec(memory_space=pl.ANY)],
-            out_specs=pl.BlockSpec(memory_space=pl.ANY),
+            in_specs=[anywhere],
+            out_specs=(anywhere, anywhere),
             scratch_shapes=[
                 pltpu.VMEM((count, block, width), jnp.float32),
                 pltpu.SemaphoreType.DMA((PACK_CHUNKS,)),
                 pltpu.SemaphoreType.DMA,
+                pltpu.SemaphoreType.DMA,
             ],
         ),
-        out_shape=jax.ShapeDtypeStruct((members, block, width), jnp.float32),
+        out_shape=(
+            jax.ShapeDtypeStruct((members, first + NOTE_ROWS, width), jnp.float32),
+            jax.ShapeDtypeStruct((members, LAST_ROWS, width), jnp.float32),
+        ),
         cost_estimate=pl.CostEstimate(flops=100000000, bytes_accessed=1 << 23, transcendentals=0),
         name="pack",
     )(dest, late)
@@ -121,33 +139,50 @@
     )(early, late)
 
 
-def mix_kernel(partial_ref, note_ref, out_ref):
+def mix_kernel(partial_ref, note_ref, first_ref, out_ref, rows, sem):
     members, _, width = partial_ref.shape
     gram_row = jnp.sum(partial_ref[:, 0, :], axis=0, keepdims=True)
     cross_row = jnp.sum(partial_ref[:, 1, :], axis=0, keepdims=True)
-    out_ref[:, 0, :] = jnp.broadcast_to(gram_row, (members, width))
-    out_ref[:, 1, :] = jnp.broadcast_to(cross_row, (members, width))
-    out_ref[:, 2, :] = note_ref[...]
-    out_ref[:, 3, :] = jnp.zeros((members, width), jnp.float32)
-
-
-def mix(partial, note):
+    rows[...] = jnp.zeros_like(rows)
+    rows[:, 0, :] = jnp.broadcast_to(gram_row, (members, width))
+    rows[:, 1, :] = jnp.broadcast_to(cross_row, (members, width))
+    rows[:, 2, :] = note_ref[...]
+    tail = pl.ds(out_ref.shape[1] - NOTE_ROWS, NOTE_ROWS)
+    copy = pltpu.make_async_copy(rows, out_ref.at[:, tail], sem)
+    copy.start()
+    copy.wait()
+
+
+def mix(partial, note, first):
     members, _, width = partial.shape
+    whole = pl.BlockSpec(memory_space=pltpu.VMEM)
+    anywhere = pl.BlockSpec(memory_space=pl.ANY)
     return pl.pallas_call(
         mix_kernel,
-        out_shape=jax.ShapeDtypeStruct((members, NOTE_ROWS, width), jnp.float32),
+        in_specs=[whole, whole, anywhere],
+        out_specs=anywhere,
+        out_shape=jax.ShapeDtypeStruct(first.shape, first.dtype),
+        scratch_shapes=[
+            pltpu.VMEM((members, NOTE_ROWS, width), jnp.float32),
+            pltpu.SemaphoreType.DMA,
+        ],
+        input_output_aliases={2: 0},
         cost_estimate=pl.CostEstimate(flops=1000000, bytes_accessed=1 << 19, transcendentals=0),
-        compiler_params=pltpu.CompilerParams(vmem_limit_bytes=4 << 20),
+        compiler_params=pltpu.CompilerParams(vmem_limit_bytes=57 << 20),
         name="mix",
-    )(partial, note)
+    )(partial, note, first)
 
 
 def dot3(a, b):
     return jnp.dot(a, b, precision=lax.Precision.HIGHEST, preferred_element_type=jnp.float32)
 
 
-def finish_kernel(row_total, stats_ref, weight_ref, operator_ref, work):
+def finish_kernel(row_total, arrived_ref, weight_ref, operator_ref, place_ref, work, stats_ref, sem):
     order = stats_ref.shape[0]
+    tail = pl.ds(arrived_ref.shape[1] - NOTE_ROWS, NOTE_ROWS)
+    copy = pltpu.make_async_copy(arrived_ref.at[:, tail], stats_ref, sem)
+    copy.start()
+    copy.wait()
     row_id = lax.broadcasted_iota(jnp.int32, (order, 1), 0)
     lane = lax.broadcasted_iota(jnp.int32, (1, 2 * order), 1)
     lane_half = lax.broadcasted_iota(jnp.int32, (1, order), 1)
@@ -176,86 +211,115 @@
     weight_ref[0:order, order:] = wlo
     weight_ref[order:, 0:order] = whi
     weight_ref[order:, order:] = wlo
-
-
-def finish(stats, row_total):
-    order = stats.shape[0]
+    note = stats_ref[:, 2, :]
+    empty = note == 0.0
+    counted = empty.astype(jnp.bfloat16)
+    below = (row_id > lane_half).astype(jnp.bfloat16)
+    earlier = jnp.dot(below, counted, preferred_element_type=jnp.float32)
+    filled = order - jnp.sum(counted.astype(jnp.float32), axis=0, keepdims=True)
+    code = jnp.where(empty, filled + earlier + CAP, note - 1.0)
+    place_ref[...] = code.T[0:1, :].astype(jnp.int32)
+
+
+def finish(arrived, row_total):
+    order = arrived.shape[0]
+    whole = pl.BlockSpec(memory_space=pltpu.VMEM)
     return pl.pallas_call(
         functools.partial(finish_kernel, float(row_total)),
+        in_specs=[pl.BlockSpec(memory_space=pl.ANY)],
+        out_specs=(whole, whole, whole),
         out_shape=(
             jax.ShapeDtypeStruct((2 * order, 2 * order), jnp.bfloat16),
             jax.ShapeDtypeStruct((order, order), jnp.float32),
-        ),
-        scratch_shapes=[pltpu.VMEM((order, 2 * order), jnp.float32)],
+            jax.ShapeDtypeStruct((1, order), jnp.int32),
+        ),
+        scratch_shapes=[
+            pltpu.VMEM((order, 2 * order), jnp.float32),
+            pltpu.VMEM((order, NOTE_ROWS, order), jnp.float32),
+            pltpu.SemaphoreType.DMA,
+        ],
         cost_estimate=pl.CostEstimate(flops=1000000000, bytes_accessed=1 << 19, transcendentals=0),
-        compiler_params=pltpu.CompilerParams(vmem_limit_bytes=4 << 20),
+        compiler_params=pltpu.CompilerParams(vmem_limit_bytes=57 << 20),
         name="finish",
-    )(stats)
-
-
-def apply_kernel(place_ref, weight_ref, arrived_ref, out_ref, buf_in, buf_out, sem_in, sem_out):
-    count, block, width = arrived_ref.shape
-    steps = count // APPLY_STEP
+    )(arrived)
+
+
+def apply_kernel(fast, stride, lo, height, place_ref, weight_ref, arrived_ref, *rest):
+    if fast:
+        out_ref, buf_out, sem_out = rest[-3:]
+        buf_in = arrived_ref
+    else:
+        out_ref, buf_out, sem_out, buf_in, sem_in = rest[-5:]
+    count, _, width = arrived_ref.shape
+    steps = count // stride
+    rows = pl.ds(lo, height)
 
     def fetch(t):
-        part = pl.ds(t * APPLY_STEP, APPLY_STEP)
-        return pltpu.make_async_copy(arrived_ref.at[part], buf_in.at[part], sem_in.at[t])
-
-    for t in range(steps):
-        fetch(t).start()
+        part = pl.ds(t * stride, stride)
+        return pltpu.make_async_copy(
+            arrived_ref.at[part, pl.ds(0, height)], buf_in.at[part], sem_in.at[t]
+        )
+
+    if not fast:
+        for t in range(steps):
+            fetch(t).start()
 
     def step(t, carry):
-        part = pl.ds(t * APPLY_STEP, APPLY_STEP)
-        fetch(t).wait()
-        hi, lo = split_pair(buf_in[part].reshape((APPLY_STEP * block, width)))
+        part = pl.ds(t * stride, stride)
+        if not fast:
+            fetch(t).wait()
+        hi, low = split_pair(buf_in[part].reshape((stride * height, width)))
         wide = jnp.dot(
-            jnp.concatenate([hi, lo], axis=1),
+            jnp.concatenate([hi, low], axis=1),
             weight_ref[...],
             preferred_element_type=jnp.float32,
         )
         solved = wide[:, 0:width] + wide[:, width:]
-        buf_out[part] = solved.reshape((APPLY_STEP, block, width))
-        for i in range(APPLY_STEP):
-            row = t * APPLY_STEP + i
+        buf_out[part] = solved.reshape((stride, height, width))
+        for i in range(stride):
+            row = t * stride + i
             code = place_ref[row]
 
             @pl.when(code >= count)
             def _():
-                buf_out[row] = jnp.zeros((block, width), jnp.float32)
+                buf_out[row] = jnp.zeros((height, width), jnp.float32)
 
             pltpu.make_async_copy(
-                buf_out.at[row], out_ref.at[lax.rem(code, count)], sem_out
+                buf_out.at[row], out_ref.at[lax.rem(code, count), rows], sem_out
             ).start()
         return carry
 
     lax.fori_loop(0, steps, step, 0)
-    pltpu.make_async_copy(buf_out, out_ref, sem_out).wait()
-
-
-def apply_inverse(place, weight, arrived):
-    count, block, width = arrived.shape
+    pltpu.make_async_copy(buf_out, out_ref.at[:, rows], sem_out).wait()
+
+
+def apply_inverse(place, weight, arrived, modes, stride, lo, height, block):
+    count, _, width = arrived.shape
     anywhere = pl.BlockSpec(memory_space=pl.ANY)
-    return pl.pallas_call(
-        apply_kernel,
+    whole = pl.BlockSpec(memory_space=pltpu.VMEM)
+    earlier = () if modes is None else (modes,)
+    fast = modes is not None
+    rows = pltpu.VMEM((count, height, width), jnp.float32)
+    scratch = [rows, pltpu.SemaphoreType.DMA]
+    if not fast:
+        scratch += [rows, pltpu.SemaphoreType.DMA((count // stride,))]
+    return pl.pallas_call(
+        functools.partial(apply_kernel, fast, stride, lo, height),
         grid_spec=pltpu.PrefetchScalarGridSpec(
             num_scalar_prefetch=1,
             grid=(1,),
-            in_specs=[pl.BlockSpec(memory_space=pltpu.VMEM), anywhere],
+            in_specs=[whole, whole if fast else anywhere] + [anywhere] * len(earlier),
             out_specs=anywhere,
-            scratch_shapes=[
-                pltpu.VMEM((count, block, width), jnp.float32),
-                pltpu.VMEM((count, block, width), jnp.float32),
-                pltpu.SemaphoreType.DMA((count // APPLY_STEP,)),
-                pltpu.SemaphoreType.DMA,
-            ],
+            scratch_shapes=scratch,
         ),
         out_shape=jax.ShapeDtypeStruct((count, block, width), jnp.float32),
+        input_output_aliases={3: 0} if earlier else {},
         cost_estimate=pl.CostEstimate(
-            flops=8 * count * block * width * width, bytes_accessed=1 << 23, transcendentals=0
-        ),
-        compiler_params=pltpu.CompilerParams(vmem_limit_bytes=24 << 20),
+            flops=8 * count * height * width * width, bytes_accessed=1 << 23, transcendentals=0
+        ),
+        compiler_params=pltpu.CompilerParams(vmem_limit_bytes=(4 if fast else 57) << 20),
         name="apply",
-    )(place, weight, arrived)
+    )(place, weight, arrived, *earlier)
 
 
 def exchange(payload):
@@ -280,19 +344,15 @@
         jnp.where(dest[None, :] == target[:, None], slot_here[None, :] + 1, 0), axis=1
     )
     note = jnp.broadcast_to(note.astype(jnp.float32)[:, None], (members, width))
-    payload = pack(snap_late, dest, members)
-    stats = exchange(mix(partial, note))
-    payload, _ = lax.optimization_barrier((payload, stats))
-    arrived = exchange(payload)
-    weight, operator = finish(stats, row_total)
-    slot_in = stats[:, 2, 0].astype(jnp.int32)
-    empty = slot_in == 0
-    filled = jnp.sum((slot_in > 0).astype(jnp.int32))
-    earlier = jnp.sum(
-        jnp.where(empty[None, :] & (target[None, :] < target[:, None]), 1, 0), axis=1
-    )
-    place = jnp.where(empty, filled + earlier + CAP, slot_in - 1)
-    modes = apply_inverse(place, weight, arrived)
+    first, last = pack(snap_late, dest, members)
+    first = exchange(mix(partial, note, first))
+    last, first = lax.optimization_barrier((last, first))
+    last = exchange(last)
+    weight, operator, place = finish(first, row_total)
+    place = place.reshape((members,))
+    height = block - LAST_ROWS
+    modes = apply_inverse(place, weight, first, None, 16, 0, height, block)
+    modes = apply_inverse(place, weight, last, modes, 64, height, LAST_ROWS, block)
     return (modes, operator)
 
 

time: 163 us -> 166 us (1.018); the launches traced: 160 us -> 166 us
  blocking collectives: 0 us -> 99.2 us
  waiting for transfers between devices: 94.1 us -> 2.6 us
  other arithmetic: 6.88 us -> 0.95 us
  Pallas kernels: 37 us -> 42.9 us
  starting transfers between devices: 21.5 us -> 17.9 us
    all_to_all x0 -> x1, blocking collectives: none -> 99.2 us  [exchange(): lax.all_to_all(payload, AXES, split_axis=0, concat_axis=0, tiled=True)]
    all_to_all x3 -> x2, waiting for transfers between devices: 94.1 us -> 2.6 us  [exchange(): lax.all_to_all(payload, AXES, split_axis=0, concat_axis=0, tiled=True)]
    pallas_call x3 -> x4, Pallas kernels: 24 us -> 29.9 us  [the longest x1 16.8 us: finish(): pl.pallas_call(functools.partial(finish_kernel, float(row_total)), in_spe...]
    all_to_all x3 -> x2, starting transfers between devices: 21.5 us -> 17.9 us  [exchange(): lax.all_to_all(payload, AXES, split_axis=0, concat_axis=0, tiled=True)]
    reduce_sum x2 -> x0, other arithmetic: 3 us -> none  [the longest x1 2.88 us: body(): filled = jnp.sum((slot_in > 0).astype(jnp.int32))]
    eq x1 -> x0, other arithmetic: 2.36 us -> none  [body(): empty = slot_in == 0]
  transfers between devices with their start and end apart: 3 -> 2, of which waited for: 3 -> 1; matrix products, arithmetic and copies ran while one was open for 4% -> 1% of each run, Pallas kernels for 13% -> 19%
where the time goes in v3:
time: 166 us
  blocking collectives  99.2 us (60%)
  Pallas kernels  42.9 us (26%)
  starting transfers between devices  17.9 us (11%)
  waiting for transfers between devices  2.6 us (2%)
    all_to_all x1, blocking collectives, exchange(): lax.all_to_all(payload, AXES, split_axis=0, concat_axis=0, tiled=True)  99.2 us
    all_to_all x2, starting transfers between devices, exchange(): lax.all_to_all(payload, AXES, split_axis=0, concat_axis=0, tiled=True)  17.9 us
    pallas_call x1, Pallas kernels, finish(): pl.pallas_call(functools.partial(finish_kernel, float(row_total)), in_spe...  16.8 us
    pallas_call x2, Pallas kernels, apply_inverse(): pl.pallas_call(functools.partial(apply_kernel, fast, stride, lo, height),...  11.2 us
    pallas_call x1, Pallas kernels, gram_pair(): pl.pallas_call(gram_kernel, in_specs=[anywhere, anywhere], out_specs=pl.B...  7.24 us
    pallas_call x1, Pallas kernels, pack(): pl.pallas_call(pack_kernel, grid_spec=pltpu.PrefetchScalarGridSpec(num_sc...  5.81 us
  transfers between devices with their start and end apart: 2, of which 1 were waited for; matrix products, arithmetic and copies ran while one was open for 1% of the time, Pallas kernels for 19%

profile of v3, /device:TPU:1, one launch (start us, length us, event | category | flops | bytes accessed | tf_op | source)
XLA Modules:
  0.0 165.5 jit_solution(18026977196762011073)
XLA Ops:
  0.6 0.0 copy-start.5
  0.6 0.0 copy-start.3
  0.7 0.0 copy-start.4
  0.7 7.2 %gram.1 = f32[128,2,128]{2,1,0:T(2,128)} custom-call(f32[96,128,128]{2,1,0:T(8,128)} %early_ref.1, f32[96,128,128]{2,1,0:T(8,128)} %late_ref.3), custom_call_target="tpu_custom_call" | custom-call | flops 2415919104 | bytes 8388608 | tf_op jit(solution)/shard_map/gram/pallas_call | solution.py:124
  7.9 11.5 %all-to-all-start = ((f32[128,2,128]{2,1,0:T(2,128)}), f32[128,2,128]{2,1,0:T(2,128)S(1)}, u32[]{:S(2)}, u32[]{:S(2)}) async-start(f32[128,2,128]{2,1,0:T(2,128)} %gram.1), calls=%async_computation | async-start | bytes 262144 | tf_op jit(solution)/shard_map/all_to_all | solution.py:326
  19.4 0.0 copy-done.3
  19.4 0.0 copy-done.4
  19.4 0.0 copy-done.5
  19.5 0.8 select_reduce_fusion
  20.3 0.0 copy-start.6
  20.3 0.1 select_reduce_fusion.1
  20.4 0.4 copy-done.6
  20.8 5.8 %pack.1 = (f32[128,120,128]{2,1,0:T(8,128)}, f32[128,16,128]{2,1,0:T(8,128)}) custom-call(s32[96]{0:T(128)} %copy-done.6, f32[96,128,128]{2,1,0:T(8,128)} %late_ref.3), custom_call_target="tpu_custom_call" | custom-call | flops 100000000 | bytes 8388608 | tf_op jit(solution)/shard_map/pack/pallas_call | solution.py:67
  26.6 2.6 %all-to-all-done.partial_ref = f32[128,2,128]{2,1,0:T(2,128)S(1)} async-done(((f32[128,2,128]{2,1,0:T(2,128)}), f32[128,2,128]{2,1,0:T(2,128)S(1)}, u32[]{:S(2)}, u32[]{:S(2)}) %all-to-all-start) | async-done | bytes 131104 | tf_op jit(solution)/shard_map/all_to_all | solution.py:326
  29.2 0.0 copy-start.2
  29.2 0.7 broadcast_in_dim.40.note_ref
  29.9 0.0 copy-done.2
  29.9 1.9 %mix.1 = f32[128,120,128]{2,1,0:T(8,128)} custom-call(f32[128,2,128]{2,1,0:T(2,128)} %copy-done.2, f32[128,128]{1,0:T(8,128)} %broadcast_in_dim.40.note_ref, f32[128,120,128]{2,1,0:T(8,128)} %get-tuple-element.14.first_ref), custom_call_target="tpu_custom_call", output_to_operand_aliasing={{}: (2, {})} | custom-call | flops 1000000 | bytes 524288 | tf_op jit(solution)/shard_map/mix/pallas_call | solution.py:160
  31.8 99.2 %all_to_all.15.arrived_ref = f32[128,120,128]{2,1,0:T(8,128)} all-to-all(f32[128,120,128]{2,1,0:T(8,128)} %mix.1), channel_id=1, replica_groups=mesh['rows'=64,'grp'=2] {'rows','grp'}, dimensions={0} | all-to-all | bytes 15728640 | tf_op jit(solution)/shard_map/all_to_all | solution.py:326
  131.0 6.4 %all-to-all-start.2 = ((f32[128,16,128]{2,1,0:T(8,128)}), f32[128,16,128]{2,1,0:T(8,128)S(1)}, u32[]{:S(2)}, u32[]{:S(2)}) async-start(f32[128,16,128]{2,1,0:T(8,128)} %get-tuple-element.18), calls=%async_computation.2 | async-start | bytes 2097152 | tf_op jit(solution)/shard_map/all_to_all | solution.py:326
  137.4 16.8 %finish.1 = (bf16[256,256]{1,0:T(8,128)(2,1)}, f32[128,128]{1,0:T(8,128)}, s32[1,128]{1,0:T(1,128)}) custom-call(f32[128,120,128]{2,1,0:T(8,128)} %all_to_all.15.arrived_ref), custom_call_target="tpu_custom_call" | custom-call | flops 1000000000 | bytes 524288 | tf_op jit(solution)/shard_map/finish/pallas_call | solution.py:227
  154.2 0.0 copy-start
  154.2 0.0 copy-start.1
  154.3 8.2 %apply.2.rest_0_ = f32[128,128,128]{2,1,0:T(8,128)} custom-call(s32[128]{0:T(128)} %bitcast.1, bf16[256,256]{1,0:T(8,128)(2,1)} %get-tuple-element.17.weight_ref, f32[128,120,128]{2,1,0:T(8,128)} %all_to_all.15.arrived_ref), custom_call_target="tpu_custom_call" | custom-call | flops 1879048192 | bytes 8388608 | tf_op jit(solution)/shard_map/apply/pallas_call | solution.py:306
  162.5 0.0 all-to-all-done.2.arrived_ref
  162.5 0.0 copy-done
  162.5 0.0 copy-done.1
  162.5 3.0 %apply.3 = f32[128,128,128]{2,1,0:T(8,128)} custom-call(s32[128]{0:T(128)S(1)} %bitcast.2, bf16[256,256]{1,0:T(8,128)(2,1)S(1)} %copy-done, f32[128,16,128]{2,1,0:T(8,128)S(1)} %all-to-all-done.2.arrived_ref, f32[128,128,128]{2,1,0:T(8,128)} %apply.2.rest_0_), custom_call_target="tpu_custom_call", output_to_operand_aliasing={{}: (3, {})} | custom-call | flops 268435456 | bytes 8388608 | tf_op jit(solution)/shard_map/apply/pallas_call | solution.py:306
  (3 shorter events, 0.0 us)
Async XLA Ops:
  0.6 18.8 %copy-start.5 = (s32[96]{0:T(128)S(1)}, s32[96]{0:T(128)}, u32[]{:S(2)}) copy-start(s32[96]{0:T(128)} %param.7) | copy-start | bytes 1156
  0.6 18.8 %copy-start.3 = (s32[12288]{0:T(1024)S(1)}, s32[12288]{0:T(1024)}, u32[]{:S(2)}) copy-start(s32[12288]{0:T(1024)} %param.9) | copy-start | bytes 147460
  0.7 18.8 %copy-start.4 = (s32[12288]{0:T(1024)S(1)}, s32[12288]{0:T(1024)}, u32[]{:S(2)}) copy-start(s32[12288]{0:T(1024)} %param.8) | copy-start | bytes 147460
  7.9 21.3 %all-to-all-start = ((f32[128,2,128]{2,1,0:T(2,128)}), f32[128,2,128]{2,1,0:T(2,128)S(1)}, u32[]{:S(2)}, u32[]{:S(2)}) async-start(f32[128,2,128]{2,1,0:T(2,128)} %gram.1), calls=%async_computation | async-start | bytes 262144 | tf_op jit(solution)/shard_map/all_to_all | solution.py:326
  20.3 0.5 copy-start.6
  29.2 0.7 copy-start.2
  131.0 31.4 %all-to-all-start.2 = ((f32[128,16,128]{2,1,0:T(8,128)}), f32[128,16,128]{2,1,0:T(8,128)S(1)}, u32[]{:S(2)}, u32[]{:S(2)}) async-start(f32[128,16,128]{2,1,0:T(8,128)} %get-tuple-element.18), calls=%async_computation.2 | async-start | bytes 2097152 | tf_op jit(solution)/shard_map/all_to_all | solution.py:326
  154.2 8.2 %copy-start = (bf16[256,256]{1,0:T(8,128)(2,1)S(1)}, bf16[256,256]{1,0:T(8,128)(2,1)}, u32[]{:S(2)}) copy-start(bf16[256,256]{1,0:T(8,128)(2,1)} %get-tuple-element.17.weight_ref) | copy-start | bytes 393220
  154.2 8.2 %copy-start.1 = (s32[1,128]{1,0:T(1,128)S(1)}, s32[1,128]{1,0:T(1,128)}, u32[]{:S(2)}) copy-start(s32[1,128]{1,0:T(1,128)} %get-tuple-element.16) | copy-start | bytes 1540

commit v4 on v3

--- a/solution.py
+++ b/solution.py
@@ -7,11 +7,12 @@
 from jax.experimental.pallas import tpu as pltpu
 from jax.sharding import PartitionSpec as P
 
-AXES = ("rows", "grp")
+AXES = ("y", "x", "z", "core")
+PLANE = ("x", "z", "core")
 GRAM_CHUNKS = (16, 32, 48)
 PACK_CHUNKS = 4
-NOTE_ROWS = 8
-LAST_ROWS = 16
+SUM_ROWS = 8
+LAST_ROWS = 32
 CAP = 128
 
 
@@ -27,15 +28,16 @@
     )
 
 
-def pack_kernel(dest_ref, late_ref, first_ref, last_ref, buf, sem_in, sem_out, sem_last):
-    count, block, _ = late_ref.shape
+def pack_kernel(lo, height, dest_ref, late_ref, out_ref, buf, sem_in, sem_out):
+    count = late_ref.shape[0]
     size = count // PACK_CHUNKS
-    last = last_ref.shape[1]
-    first = block - last
+    rows = pl.ds(0, height)
 
     def load(t):
         part = pl.ds(t * size, size)
-        return pltpu.make_async_copy(late_ref.at[part], buf.at[part], sem_in.at[t])
+        return pltpu.make_async_copy(
+            late_ref.at[part, pl.ds(lo, height)], buf.at[part], sem_in.at[t]
+        )
 
     for t in range(PACK_CHUNKS):
         load(t).start()
@@ -43,45 +45,30 @@
         load(t).wait()
 
         def send(i, carry):
-            row = dest_ref[i]
-            pltpu.make_async_copy(
-                buf.at[i, pl.ds(0, first)], first_ref.at[row, pl.ds(0, first)], sem_out
-            ).start()
-            pltpu.make_async_copy(
-                buf.at[i, pl.ds(first, last)], last_ref.at[row], sem_last
-            ).start()
+            pltpu.make_async_copy(buf.at[i], out_ref.at[dest_ref[i], rows], sem_out).start()
             return carry
 
         lax.fori_loop(t * size, t * size + size, send, 0, unroll=8)
-    every = pl.ds(0, count)
-    pltpu.make_async_copy(
-        buf.at[:, pl.ds(0, first)], first_ref.at[every, pl.ds(0, first)], sem_out
-    ).wait()
-    pltpu.make_async_copy(buf.at[:, pl.ds(first, last)], last_ref.at[every], sem_last).wait()
-
-
-def pack(late, dest, members):
-    count, block, width = late.shape
+    pltpu.make_async_copy(buf, out_ref.at[pl.ds(0, count), rows], sem_out).wait()
+
+
+def pack(late, dest, members, lo, height, spare):
+    count, _, width = late.shape
     anywhere = pl.BlockSpec(memory_space=pl.ANY)
-    first = block - LAST_ROWS
-    return pl.pallas_call(
-        pack_kernel,
+    return pl.pallas_call(
+        functools.partial(pack_kernel, lo, height),
         grid_spec=pltpu.PrefetchScalarGridSpec(
             num_scalar_prefetch=1,
             grid=(1,),
             in_specs=[anywhere],
-            out_specs=(anywhere, anywhere),
+            out_specs=anywhere,
             scratch_shapes=[
-                pltpu.VMEM((count, block, width), jnp.float32),
+                pltpu.VMEM((count, height, width), jnp.float32),
                 pltpu.SemaphoreType.DMA((PACK_CHUNKS,)),
                 pltpu.SemaphoreType.DMA,
-                pltpu.SemaphoreType.DMA,
             ],
         ),
-        out_shape=(
-            jax.ShapeDtypeStruct((members, first + NOTE_ROWS, width), jnp.float32),
-            jax.ShapeDtypeStruct((members, LAST_ROWS, width), jnp.float32),
-        ),
+        out_shape=jax.ShapeDtypeStruct((members, height + spare, width), jnp.float32),
         cost_estimate=pl.CostEstimate(flops=100000000, bytes_accessed=1 << 23, transcendentals=0),
         name="pack",
     )(dest, late)
@@ -111,10 +98,15 @@
         gram_wide = gram_part if gram_wide is None else gram_wide + gram_part
         cross_wide = cross_part if cross_wide is None else cross_wide + cross_part
     mixed = gram_wide[:, width:]
-    out_ref[:, 0, :] = gram_wide[:, 0:width] + (mixed + mixed.T)
-    out_ref[:, 1, :] = cross_wide[0:width, 0:width] + (
+    gram = gram_wide[:, 0:width] + (mixed + mixed.T)
+    cross = cross_wide[0:width, 0:width] + (
         cross_wide[0:width, width:] + cross_wide[width:, 0:width]
     )
+    size = out_ref.shape[0]
+    half = SUM_ROWS // 2
+    for r in range(half):
+        out_ref[:, r, :] = gram[r * size : (r + 1) * size, :]
+        out_ref[:, half + r, :] = cross[r * size : (r + 1) * size, :]
 
 
 def gram_pair(early, late):
@@ -125,7 +117,7 @@
         gram_kernel,
         in_specs=[anywhere, anywhere],
         out_specs=pl.BlockSpec(memory_space=pltpu.VMEM),
-        out_shape=jax.ShapeDtypeStruct((width, 2, width), jnp.float32),
+        out_shape=jax.ShapeDtypeStruct((2 * width // SUM_ROWS, SUM_ROWS, width), jnp.float32),
         scratch_shapes=[
             pltpu.VMEM((count, block, width), jnp.float32),
             pltpu.VMEM((count, block, width), jnp.float32),
@@ -140,21 +132,20 @@
 
 
 def mix_kernel(partial_ref, note_ref, first_ref, out_ref, rows, sem):
-    members, _, width = partial_ref.shape
-    gram_row = jnp.sum(partial_ref[:, 0, :], axis=0, keepdims=True)
-    cross_row = jnp.sum(partial_ref[:, 1, :], axis=0, keepdims=True)
-    rows[...] = jnp.zeros_like(rows)
-    rows[:, 0, :] = jnp.broadcast_to(gram_row, (members, width))
-    rows[:, 1, :] = jnp.broadcast_to(cross_row, (members, width))
-    rows[:, 2, :] = note_ref[...]
-    tail = pl.ds(out_ref.shape[1] - NOTE_ROWS, NOTE_ROWS)
+    members, _, width = rows.shape
+    total = jnp.sum(partial_ref[...], axis=0, keepdims=True)
+    rows[...] = jnp.broadcast_to(total, rows.shape)
+    mark = SUM_ROWS // 2 - 1
+    lane = lax.broadcasted_iota(jnp.int32, (members, width), 1)
+    rows[:, mark, :] = jnp.where(lane == 0, note_ref[...], total[0, mark : mark + 1, :])
+    tail = pl.ds(out_ref.shape[1] - SUM_ROWS, SUM_ROWS)
     copy = pltpu.make_async_copy(rows, out_ref.at[:, tail], sem)
     copy.start()
     copy.wait()
 
 
 def mix(partial, note, first):
-    members, _, width = partial.shape
+    members, _, width = first.shape
     whole = pl.BlockSpec(memory_space=pltpu.VMEM)
     anywhere = pl.BlockSpec(memory_space=pl.ANY)
     return pl.pallas_call(
@@ -163,7 +154,7 @@
         out_specs=anywhere,
         out_shape=jax.ShapeDtypeStruct(first.shape, first.dtype),
         scratch_shapes=[
-            pltpu.VMEM((members, NOTE_ROWS, width), jnp.float32),
+            pltpu.VMEM((members, SUM_ROWS, width), jnp.float32),
             pltpu.SemaphoreType.DMA,
         ],
         input_output_aliases={2: 0},
@@ -179,14 +170,22 @@
 
 def finish_kernel(row_total, arrived_ref, weight_ref, operator_ref, place_ref, work, stats_ref, sem):
     order = stats_ref.shape[0]
-    tail = pl.ds(arrived_ref.shape[1] - NOTE_ROWS, NOTE_ROWS)
+    tail = pl.ds(arrived_ref.shape[1] - SUM_ROWS, SUM_ROWS)
     copy = pltpu.make_async_copy(arrived_ref.at[:, tail], stats_ref, sem)
     copy.start()
     copy.wait()
     row_id = lax.broadcasted_iota(jnp.int32, (order, 1), 0)
     lane = lax.broadcasted_iota(jnp.int32, (1, 2 * order), 1)
     lane_half = lax.broadcasted_iota(jnp.int32, (1, order), 1)
-    work[:, 0:order] = stats_ref[:, 0, :] / row_total
+    size = 2 * order // SUM_ROWS
+    half = SUM_ROWS // 2
+    note = stats_ref[:, half - 1, 0:1]
+    total = stats_ref[0:size]
+    for p in range(1, order // size):
+        total = total + stats_ref[p * size : (p + 1) * size]
+    gram = jnp.concatenate([total[:, r, :] for r in range(half)], axis=0)
+    cross = jnp.concatenate([total[:, half + r, :] for r in range(half)], axis=0) / row_total
+    work[:, 0:order] = jnp.where(row_id > lane_half, gram.T, gram) / row_total
     work[:, order:] = (row_id == lane_half).astype(jnp.float32)
 
     def step(j, carry):
@@ -204,14 +203,13 @@
     lax.fori_loop(0, order, step, 0)
     inverse_t = work[:, order:]
     inverse = inverse_t.T
-    cross = stats_ref[:, 1, :] / row_total
     operator_ref[...] = dot3(inverse_t, dot3(cross, inverse))
     whi, wlo = split_pair(inverse)
     weight_ref[0:order, 0:order] = whi
     weight_ref[0:order, order:] = wlo
     weight_ref[order:, 0:order] = whi
     weight_ref[order:, order:] = wlo
-    note = stats_ref[:, 2, :]
+    note = jnp.broadcast_to(note, (order, order))
     empty = note == 0.0
     counted = empty.astype(jnp.bfloat16)
     below = (row_id > lane_half).astype(jnp.bfloat16)
@@ -235,7 +233,7 @@
         ),
         scratch_shapes=[
             pltpu.VMEM((order, 2 * order), jnp.float32),
-            pltpu.VMEM((order, NOTE_ROWS, order), jnp.float32),
+            pltpu.VMEM((order, SUM_ROWS, order), jnp.float32),
             pltpu.SemaphoreType.DMA,
         ],
         cost_estimate=pl.CostEstimate(flops=1000000000, bytes_accessed=1 << 19, transcendentals=0),
@@ -322,8 +320,8 @@
     )(place, weight, arrived, *earlier)
 
 
-def exchange(payload):
-    return lax.all_to_all(payload, AXES, split_axis=0, concat_axis=0, tiled=True)
+def exchange(payload, axes=AXES):
+    return lax.all_to_all(payload, axes, split_axis=0, concat_axis=0, tiled=True)
 
 
 def body(snap_early, snap_late, block_ids, block_owner, block_slot):
@@ -332,7 +330,7 @@
     row_total = count * block * members
     outgoing = gram_pair(snap_early, snap_late)
     block_ids, outgoing = lax.optimization_barrier((block_ids, outgoing))
-    partial = exchange(outgoing)
+    partial = exchange(outgoing, PLANE)
     labels = jnp.arange(block_owner.shape[0], dtype=jnp.int32)
     code = block_owner * CAP + block_slot
     hits = block_ids[:, None] == labels[None, :]
@@ -344,19 +342,23 @@
         jnp.where(dest[None, :] == target[:, None], slot_here[None, :] + 1, 0), axis=1
     )
     note = jnp.broadcast_to(note.astype(jnp.float32)[:, None], (members, width))
-    first, last = pack(snap_late, dest, members)
-    first = exchange(mix(partial, note, first))
+    height = block - LAST_ROWS
+    first = pack(snap_late, dest, members, 0, height, SUM_ROWS)
+    first = mix(partial, note, first)
+    dest, first = lax.optimization_barrier((dest, first))
+    first = exchange(first)
+    last = pack(snap_late, dest, members, height, LAST_ROWS, 0)
     last, first = lax.optimization_barrier((last, first))
     last = exchange(last)
     weight, operator, place = finish(first, row_total)
     place = place.reshape((members,))
-    height = block - LAST_ROWS
     modes = apply_inverse(place, weight, first, None, 16, 0, height, block)
     modes = apply_inverse(place, weight, last, modes, 64, height, LAST_ROWS, block)
     return (modes, operator)
 
 
 def solution(mesh):
+    split = jax.sharding.Mesh(mesh.devices.reshape((4, 4, 4, 2)), AXES)
     placed = (
         P(AXES, None, None),
         P(AXES, None, None),
@@ -366,7 +368,7 @@
     )
     return jax.shard_map(
         body,
-        mesh=mesh,
+        mesh=split,
         in_specs=placed,
         out_specs=(P(AXES, None, None), P()),
         check_vma=False,

time: 166 us -> 162 us (0.976)
  blocking collectives: 99.2 us -> 0 us
  waiting for transfers between devices: 2.6 us -> 86.7 us
  starting transfers between devices: 17.9 us -> 28 us
    all_to_all x1 -> x0, blocking collectives: 99.2 us -> none  [exchange(): lax.all_to_all(payload, AXES, split_axis=0, concat_axis=0, tiled=True)]
    all_to_all x2 -> x3, waiting for transfers between devices: 2.6 us -> 86.7 us  [exchange(): lax.all_to_all(payload, axes, split_axis=0, concat_axis=0, tiled=True)]
    all_to_all x2 -> x3, starting transfers between devices: 17.9 us -> 28 us  [exchange(): lax.all_to_all(payload, axes, split_axis=0, concat_axis=0, tiled=True)]
    pallas_call x1 -> x2, Pallas kernels: 5.81 us -> 7.22 us  [pack(): pl.pallas_call(functools.partial(pack_kernel, lo, height), grid_spec=pltp...]
  transfers between devices with their start and end apart: 2 -> 3, of which waited for: 1 -> 3; matrix products, arithmetic and copies ran while one was open for 1% -> 1% of each run, Pallas kernels for 19% -> 20%
where the time goes in v4:
time: 162 us
  waiting for transfers between devices  86.7 us (54%)
  Pallas kernels  44.3 us (27%)
  starting transfers between devices  28 us (17%)
    all_to_all x3, waiting for transfers between devices, exchange(): lax.all_to_all(payload, axes, split_axis=0, concat_axis=0, tiled=True)  86.7 us
    all_to_all x3, starting transfers between devices, exchange(): lax.all_to_all(payload, axes, split_axis=0, concat_axis=0, tiled=True)  28 us
    pallas_call x1, Pallas kernels, finish(): pl.pallas_call(functools.partial(finish_kernel, float(row_total)), in_spe...  16.9 us
    pallas_call x2, Pallas kernels, apply_inverse(): pl.pallas_call(functools.partial(apply_kernel, fast, stride, lo, height),...  11.2 us
    pallas_call x1, Pallas kernels, gram_pair(): pl.pallas_call(gram_kernel, in_specs=[anywhere, anywhere], out_specs=pl.B...  7.24 us
    pallas_call x2, Pallas kernels, pack(): pl.pallas_call(functools.partial(pack_kernel, lo, height), grid_spec=pltp...  7.22 us
  transfers between devices with their start and end apart: 3, of which 3 were waited for; matrix products, arithmetic and copies ran while one was open for 1% of the time, Pallas kernels for 20%

profile of v4, /device:TPU:1, one launch (start us, length us, event | category | flops | bytes accessed | tf_op | source)
XLA Modules:
  0.0 161.8 jit_solution(11081233103657462080)
XLA Ops:
  0.6 0.0 copy-start.6
  0.6 0.0 copy-start.3
  0.7 0.0 copy-start.4
  0.7 7.2 %gram.1 = f32[32,8,128]{2,1,0:T(8,128)} custom-call(f32[96,128,128]{2,1,0:T(8,128)} %early_ref.1, f32[96,128,128]{2,1,0:T(8,128)} %late_ref.5), custom_call_target="tpu_custom_call" | custom-call | flops 2415919104 | bytes 8388608 | tf_op jit(solution)/shard_map/gram/pallas_call | solution.py:116
  7.9 9.4 %all-to-all-start = ((f32[32,8,128]{2,1,0:T(8,128)}), f32[32,8,128]{2,1,0:T(8,128)S(1)}, u32[]{:S(2)}, u32[]{:S(2)}) async-start(f32[32,8,128]{2,1,0:T(8,128)} %gram.1), calls=%async_computation | async-start | bytes 262144 | tf_op jit(solution)/shard_map/all_to_all | solution.py:324
  17.4 0.0 copy-done.3
  17.4 0.0 copy-done.4
  17.4 0.0 copy-done.6
  17.4 0.8 select_reduce_fusion
  18.2 0.0 copy-start.5
  18.2 0.1 select_reduce_fusion.1
  18.4 0.4 copy-done.5
  18.7 4.3 %pack.2.first_ref = f32[128,104,128]{2,1,0:T(8,128)} custom-call(s32[96]{0:T(128)} %copy-done.5, f32[96,128,128]{2,1,0:T(8,128)} %late_ref.5), custom_call_target="tpu_custom_call" | custom-call | flops 100000000 | bytes 8388608 | tf_op jit(solution)/shard_map/pack/pallas_call | solution.py:58
  23.1 2.0 %all-to-all-done.partial_ref = f32[32,8,128]{2,1,0:T(8,128)S(1)} async-done(((f32[32,8,128]{2,1,0:T(8,128)}), f32[32,8,128]{2,1,0:T(8,128)S(1)}, u32[]{:S(2)}, u32[]{:S(2)}) %all-to-all-start) | async-done | bytes 131104 | tf_op jit(solution)/shard_map/all_to_all | solution.py:324
  25.0 0.0 copy-start.2
  25.0 0.7 broadcast_in_dim.40.note_ref
  25.7 0.0 copy-done.2
  25.7 1.8 %mix.1 = f32[128,104,128]{2,1,0:T(8,128)} custom-call(f32[32,8,128]{2,1,0:T(8,128)} %copy-done.2, f32[128,128]{1,0:T(8,128)} %broadcast_in_dim.40.note_ref, f32[128,104,128]{2,1,0:T(8,128)} %pack.2.first_ref), custom_call_target="tpu_custom_call", output_to_operand_aliasing={{}: (2, {})} | custom-call | flops 1000000 | bytes 524288 | tf_op jit(solution)/shard_map/mix/pallas_call | solution.py:151
  27.6 7.9 %all-to-all-start.1 = ((f32[128,104,128]{2,1,0:T(8,128)}), f32[128,104,128]{2,1,0:T(8,128)}, u32[]{:S(2)}, u32[]{:S(2)}) async-start(f32[128,104,128]{2,1,0:T(8,128)} %mix.1), calls=%async_computation.1 | async-start | bytes 13631488 | tf_op jit(solution)/shard_map/all_to_all | solution.py:324
  35.5 2.9 %pack.3 = f32[128,32,128]{2,1,0:T(8,128)} custom-call(s32[96]{0:T(128)} %copy-done.5, f32[96,128,128]{2,1,0:T(8,128)} %late_ref.5), custom_call_target="tpu_custom_call" | custom-call | flops 100000000 | bytes 8388608 | tf_op jit(solution)/shard_map/pack/pallas_call | solution.py:58
  38.4 79.4 %all-to-all-done.1.arrived_ref = f32[128,104,128]{2,1,0:T(8,128)} async-done(((f32[128,104,128]{2,1,0:T(8,128)}), f32[128,104,128]{2,1,0:T(8,128)}, u32[]{:S(2)}, u32[]{:S(2)}) %all-to-all-start.1) | async-done | bytes 6815776 | tf_op jit(solution)/shard_map/all_to_all | solution.py:324
  117.8 10.6 %all-to-all-start.2 = ((f32[128,32,128]{2,1,0:T(8,128)}), f32[128,32,128]{2,1,0:T(8,128)S(1)}, u32[]{:S(2)}, u32[]{:S(2)}) async-start(f32[128,32,128]{2,1,0:T(8,128)} %pack.3), calls=%async_computation.2 | async-start | bytes 4194304 | tf_op jit(solution)/shard_map/all_to_all | solution.py:324
  128.4 16.9 %finish.1 = (bf16[256,256]{1,0:T(8,128)(2,1)}, f32[128,128]{1,0:T(8,128)}, s32[1,128]{1,0:T(1,128)}) custom-call(f32[128,104,128]{2,1,0:T(8,128)} %all-to-all-done.1.arrived_ref), custom_call_target="tpu_custom_call" | custom-call | flops 1000000000 | bytes 524288 | tf_op jit(solution)/shard_map/finish/pallas_call | solution.py:225
  145.3 0.0 copy-start
  145.3 0.0 copy-start.1
  145.3 7.8 %apply.2.rest_0_ = f32[128,128,128]{2,1,0:T(8,128)} custom-call(s32[128]{0:T(128)} %bitcast.1, bf16[256,256]{1,0:T(8,128)(2,1)} %get-tuple-element.17.weight_ref, f32[128,104,128]{2,1,0:T(8,128)} %all-to-all-done.1.arrived_ref), custom_call_target="tpu_custom_call" | custom-call | flops 1610612736 | bytes 8388608 | tf_op jit(solution)/shard_map/apply/pallas_call | solution.py:304
  153.2 5.3 %all-to-all-done.2.arrived_ref = f32[128,32,128]{2,1,0:T(8,128)S(1)} async-done(((f32[128,32,128]{2,1,0:T(8,128)}), f32[128,32,128]{2,1,0:T(8,128)S(1)}, u32[]{:S(2)}, u32[]{:S(2)}) %all-to-all-start.2) | async-done | bytes 2097184 | tf_op jit(solution)/shard_map/all_to_all | solution.py:324
  158.5 0.0 copy-done
  158.5 0.0 copy-done.1
  158.5 3.3 %apply.3 = f32[128,128,128]{2,1,0:T(8,128)} custom-call(s32[128]{0:T(128)S(1)} %bitcast.2, bf16[256,256]{1,0:T(8,128)(2,1)S(1)} %copy-done, f32[128,32,128]{2,1,0:T(8,128)S(1)} %all-to-all-done.2.arrived_ref, f32[128,128,128]{2,1,0:T(8,128)} %apply.2.rest_0_), custom_call_target="tpu_custom_call", output_to_operand_aliasing={{}: (3, {})} | custom-call | flops 536870912 | bytes 8388608 | tf_op jit(solution)/shard_map/apply/pallas_call | solution.py:304
  (3 shorter events, 0.0 us)
Async XLA Ops:
  0.6 16.8 %copy-start.6 = (s32[96]{0:T(128)S(1)}, s32[96]{0:T(128)}, u32[]{:S(2)}) copy-start(s32[96]{0:T(128)} %param.7) | copy-start | bytes 1156
  0.6 16.7 %copy-start.3 = (s32[12288]{0:T(1024)S(1)}, s32[12288]{0:T(1024)}, u32[]{:S(2)}) copy-start(s32[12288]{0:T(1024)} %param.9) | copy-start | bytes 147460
  0.7 16.7 %copy-start.4 = (s32[12288]{0:T(1024)S(1)}, s32[12288]{0:T(1024)}, u32[]{:S(2)}) copy-start(s32[12288]{0:T(1024)} %param.8) | copy-start | bytes 147460
  7.9 17.1 %all-to-all-start = ((f32[32,8,128]{2,1,0:T(8,128)}), f32[32,8,128]{2,1,0:T(8,128)S(1)}, u32[]{:S(2)}, u32[]{:S(2)}) async-start(f32[32,8,128]{2,1,0:T(8,128)} %gram.1), calls=%async_computation | async-start | bytes 262144 | tf_op jit(solution)/shard_map/all_to_all | solution.py:324
  18.2 0.5 copy-start.5
  25.0 0.7 copy-start.2
  27.6 90.2 %all-to-all-start.1 = ((f32[128,104,128]{2,1,0:T(8,128)}), f32[128,104,128]{2,1,0:T(8,128)}, u32[]{:S(2)}, u32[]{:S(2)}) async-start(f32[128,104,128]{2,1,0:T(8,128)} %mix.1), calls=%async_computation.1 | async-start | bytes 13631488 | tf_op jit(solution)/shard_map/all_to_all | solution.py:324
  117.8 40.8 %all-to-all-start.2 = ((f32[128,32,128]{2,1,0:T(8,128)}), f32[128,32,128]{2,1,0:T(8,128)S(1)}, u32[]{:S(2)}, u32[]{:S(2)}) async-start(f32[128,32,128]{2,1,0:T(8,128)} %pack.3), calls=%async_computation.2 | async-start | bytes 4194304 | tf_op jit(solution)/shard_map/all_to_all | solution.py:324
  145.3 13.2 %copy-start = (bf16[256,256]{1,0:T(8,128)(2,1)S(1)}, bf16[256,256]{1,0:T(8,128)(2,1)}, u32[]{:S(2)}) copy-start(bf16[256,256]{1,0:T(8,128)(2,1)} %get-tuple-element.17.weight_ref) | copy-start | bytes 393220
  145.3 13.2 %copy-start.1 = (s32[1,128]{1,0:T(1,128)S(1)}, s32[1,128]{1,0:T(1,128)}, u32[]{:S(2)}) copy-start(s32[1,128]{1,0:T(1,128)} %get-tuple-element.16) | copy-start | bytes 1540

commit v5 on v4

v5 whole, which is shorter than its diff:
```python
import functools

import jax
import jax.numpy as jnp
from jax import lax
from jax.experimental import pallas as pl
from jax.experimental.pallas import tpu as pltpu
from jax.sharding import PartitionSpec as P

AXES = ("y", "x", "z", "core")
PLANE = ("x", "z", "core")
GRAM_CHUNKS = (16, 32, 48)
PACK_CHUNKS = 4
APPLY_STEP = 16
SUM_ROWS = 8
PIVOTS = 4
SHRINK = 32
CAP = 128


def split_pair(x):
    hi = x.astype(jnp.bfloat16)
    lo = (x - hi.astype(jnp.float32)).astype(jnp.bfloat16)
    return hi, lo


def contract_rows(a, b):
    return lax.dot_general(
        a, b, (((0,), (0,)), ((), ())), preferred_element_type=jnp.float32
    )


def pack_kernel(lo, height, dest_ref, late_ref, out_ref, buf, sem_in, sem_out):
    count = late_ref.shape[0]
    size = count // PACK_CHUNKS
    rows = pl.ds(0, height)

    def load(t):
        part = pl.ds(t * size, size)
        return pltpu.make_async_copy(
            late_ref.at[part, pl.ds(lo, height)], buf.at[part], sem_in.at[t]
        )

    for t in range(PACK_CHUNKS):
        load(t).start()
    for t in range(PACK_CHUNKS):
        load(t).wait()

        def send(i, carry):
            pltpu.make_async_copy(buf.at[i], out_ref.at[dest_ref[i], rows], sem_out).start()
            return carry

        lax.fori_loop(t * size, t * size + size, send, 0, unroll=8)
    pltpu.make_async_copy(buf, out_ref.at[pl.ds(0, count), rows], sem_out).wait()


def pack(late, dest, members, lo, height, spare):
    count, _, width = late.shape
    anywhere = pl.BlockSpec(memory_space=pl.ANY)
    return pl.pallas_call(
        functools.partial(pack_kernel, lo, height),
        grid_spec=pltpu.PrefetchScalarGridSpec(
            num_scalar_prefetch=1,
            grid=(1,),
            in_specs=[anywhere],
            out_specs=anywhere,
            scratch_shapes=[
                pltpu.VMEM((count, height, width), jnp.float32),
                pltpu.SemaphoreType.DMA((PACK_CHUNKS,)),
                pltpu.SemaphoreType.DMA,
            ],
        ),
        out_shape=jax.ShapeDtypeStruct((members, height + spare, width), jnp.float32),
        cost_estimate=pl.CostEstimate(flops=100000000, bytes_accessed=1 << 23, transcendentals=0),
        name="pack",
    )(dest, late)


def gram_kernel(early_ref, late_ref, out_ref, early_buf, late_buf, sem_early, sem_late):
    width = early_ref.shape[2]
    parts = []
    lo = 0
    for k, size in enumerate(GRAM_CHUNKS):
        part = pl.ds(lo, size)
        one = pltpu.make_async_copy(early_ref.at[part], early_buf.at[part], sem_early.at[k])
        two = pltpu.make_async_copy(late_ref.at[part], late_buf.at[part], sem_late.at[k])
        one.start()
        two.start()
        parts.append((part, one, two))
        lo += size
    gram_wide = cross_wide = None
    for part, one, two in parts:
        one.wait()
        two.wait()
        ehi, elo = split_pair(early_buf[part].reshape((-1, width)))
        lhi, llo = split_pair(late_buf[part].reshape((-1, width)))
        pair = jnp.concatenate([ehi, elo], axis=1)
        gram_part = contract_rows(ehi, pair)
        cross_part = contract_rows(pair, jnp.concatenate([lhi, llo], axis=1))
        gram_wide = gram_part if gram_wide is None else gram_wide + gram_part
        cross_wide = cross_part if cross_wide is None else cross_wide + cross_part
    mixed = gram_wide[:, width:]
    gram = gram_wide[:, 0:width] + (mixed + mixed.T)
    cross = cross_wide[0:width, 0:width] + (
        cross_wide[0:width, width:] + cross_wide[width:, 0:width]
    )
    size = out_ref.shape[0]
    half = SUM_ROWS // 2
    for r in range(half):
        out_ref[:, r, :] = gram[r * size : (r + 1) * size, :]
        out_ref[:, half + r, :] = cross[r * size : (r + 1) * size, :]


def gram_pair(early, late):
    count, block, width = early.shape
    steps = len(GRAM_CHUNKS)
    anywhere = pl.BlockSpec(memory_space=pl.ANY)
    return pl.pallas_call(
        gram_kernel,
        in_specs=[anywhere, anywhere],
        out_specs=pl.BlockSpec(memory_space=pltpu.VMEM),
        out_shape=jax.ShapeDtypeStruct((2 * width // SUM_ROWS, SUM_ROWS, width), jnp.float32),
        scratch_shapes=[
            pltpu.VMEM((count, block, width), jnp.float32),
            pltpu.VMEM((count, block, width), jnp.float32),
            pltpu.SemaphoreType.DMA((steps,)),
            pltpu.SemaphoreType.DMA((steps,)),
        ],
        cost_estimate=pl.CostEstimate(
            flops=12 * count * block * width * width, bytes_accessed=1 << 23, transcendentals=0
        ),
        name="gram",
    )(early, late)


def mix_kernel(partial_ref, code_ref, first_ref, out_ref, rows, sem):
    members, _, width = rows.shape
    total = jnp.sum(partial_ref[...], axis=0, keepdims=True)
    rows[...] = jnp.broadcast_to(total, rows.shape)
    mark = SUM_ROWS // 2 - 1
    code = code_ref[...]
    peer = lax.broadcasted_iota(jnp.int32, (members, code.shape[1]), 0)
    slot = (jnp.bitwise_and(code, CAP - 1) + 1).astype(jnp.float32)
    here = jnp.where(jnp.right_shift(code, 7) == peer, slot, 0.0)
    note = jnp.sum(here, axis=1, keepdims=True)
    lane = lax.broadcasted_iota(jnp.int32, (members, width), 1)
    rows[:, mark, :] = jnp.where(lane == 0, note, total[0, mark : mark + 1, :])
    tail = pl.ds(out_ref.shape[1] - SUM_ROWS, SUM_ROWS)
    copy = pltpu.make_async_copy(rows, out_ref.at[:, tail], sem)
    copy.start()
    copy.wait()


def mix(partial, code, first):
    members, _, width = first.shape
    whole = pl.BlockSpec(memory_space=pltpu.VMEM)
    anywhere = pl.BlockSpec(memory_space=pl.ANY)
    return pl.pallas_call(
        mix_kernel,
        in_specs=[whole, whole, anywhere],
        out_specs=anywhere,
        out_shape=jax.ShapeDtypeStruct(first.shape, first.dtype),
        scratch_shapes=[
            pltpu.VMEM((members, SUM_ROWS, width), jnp.float32),
            pltpu.SemaphoreType.DMA,
        ],
        input_output_aliases={2: 0},
        cost_estimate=pl.CostEstimate(flops=1000000, bytes_accessed=1 << 19, transcendentals=0),
        compiler_params=pltpu.CompilerParams(vmem_limit_bytes=57 << 20),
        name="mix",
    )(partial, code, first)


def dot3(a, b):
    return jnp.dot(a, b, precision=lax.Precision.HIGHEST, preferred_element_type=jnp.float32)


def eliminate(work):
    order = work.shape[0]
    lane = lax.broadcasted_iota(jnp.int32, (1, 2 * order), 1)
    lane_half = lax.broadcasted_iota(jnp.int32, (1, order), 1)

    def step(lo, k, carry):
        j = lo + k * PIVOTS
        row_id = lo + lax.broadcasted_iota(jnp.int32, (order - lo, 1), 0)
        table = work[lo:order, :]
        left = table[:, 0:order]
        rows = []
        columns = []
        for p in range(PIVOTS):
            rows.append(work[pl.ds(j + p, 1), :])
            picked = jnp.where(lane_half == j + p, left, 0.0)
            columns.append(jnp.sum(picked, axis=1, keepdims=True))
        block = {}
        for p in range(PIVOTS):
            for q in range(p, PIVOTS):
                picked = jnp.where(lane == j + q, rows[p], 0.0)
                block[p, q] = jnp.sum(picked, axis=1, keepdims=True)
        upper = {}
        for p in range(PIVOTS):
            pivot = block[p, p]
            for m in range(p):
                pivot = pivot - upper[m, p] * upper[m, p]
            inv = lax.rsqrt(pivot)
            for q in range(p + 1, PIVOTS):
                entry = block[p, q]
                for m in range(p):
                    entry = entry - upper[m, p] * upper[m, q]
                upper[p, q] = entry * inv
            for m in range(p):
                rows[p] = rows[p] - upper[m, p] * rows[m]
                columns[p] = columns[p] - upper[m, p] * columns[m]
            rows[p] = rows[p] * inv
            columns[p] = columns[p] * inv
        below = row_id >= j + PIVOTS
        for p in range(PIVOTS):
            table = table - jnp.where(below, columns[p], 0.0) * rows[p]
        for p in range(PIVOTS):
            table = jnp.where(row_id == j + p, rows[p], table)
        work[lo:order, :] = table
        return carry

    for lo in range(0, order, SHRINK):
        lax.fori_loop(0, SHRINK // PIVOTS, functools.partial(step, lo), 0)


def settle_kernel(
    row_total,
    arrived_ref,
    modes_ref,
    operator_ref,
    buf_in,
    buf_out,
    stats_ref,
    work,
    weight_ref,
    place_ref,
    slots_ref,
    sem_stats,
    sem_in,
    sem_out,
    sem_place,
):
    count, block, width = modes_ref.shape
    order = width
    steps = count // APPLY_STEP
    stats_copy = pltpu.make_async_copy(
        arrived_ref.at[:, pl.ds(block, SUM_ROWS)], stats_ref, sem_stats
    )
    stats_copy.start()

    def fetch(t):
        part = pl.ds(t * APPLY_STEP, APPLY_STEP)
        return pltpu.make_async_copy(
            arrived_ref.at[part, pl.ds(0, block)], buf_in.at[part], sem_in.at[t]
        )

    for t in range(steps):
        fetch(t).start()
    stats_copy.wait()

    row_id = lax.broadcasted_iota(jnp.int32, (order, 1), 0)
    lane = lax.broadcasted_iota(jnp.int32, (1, order), 1)
    size = 2 * order // SUM_ROWS
    half = SUM_ROWS // 2
    total = stats_ref[0:size]
    for p in range(1, order // size):
        total = total + stats_ref[p * size : (p + 1) * size]
    gram = jnp.concatenate([total[:, r, :] for r in range(half)], axis=0)
    work[:, 0:order] = jnp.where(row_id > lane, gram.T, gram) / row_total
    work[:, order:] = (row_id == lane).astype(jnp.float32)

    note = jnp.broadcast_to(stats_ref[:, half - 1, 0:1], (count, count))
    empty = note == 0.0
    counted = empty.astype(jnp.bfloat16)
    below = (row_id > lane).astype(jnp.bfloat16)
    earlier = jnp.dot(below, counted, preferred_element_type=jnp.float32)
    filled = count - jnp.sum(counted.astype(jnp.float32), axis=0, keepdims=True)
    code = jnp.where(empty, filled + earlier + CAP, note - 1.0)
    place_ref[...] = code.T[0:1, :].astype(jnp.int32)
    place_copy = pltpu.make_async_copy(place_ref, slots_ref, sem_place)
    place_copy.start()

    eliminate(work)
    inverse_t = work[:, order:]
    inverse = inverse_t.T
    whi, wlo = split_pair(inverse)
    weight_ref[0:order, 0:order] = whi
    weight_ref[0:order, order:] = wlo
    weight_ref[order:, 0:order] = whi
    weight_ref[order:, order:] = wlo
    place_copy.wait()

    def step(t, carry):
        part = pl.ds(t * APPLY_STEP, APPLY_STEP)
        fetch(t).wait()
        hi, low = split_pair(buf_in[part].reshape((APPLY_STEP * block, width)))
        wide = jnp.dot(
            jnp.concatenate([hi, low], axis=1),
            weight_ref[...],
            preferred_element_type=jnp.float32,
        )
        solved = wide[:, 0:width] + wide[:, width:]
        buf_out[part] = solved.reshape((APPLY_STEP, block, width))
        for i in range(APPLY_STEP):
            row = t * APPLY_STEP + i
            slot = slots_ref[0, row]

            @pl.when(slot >= CAP)
            def _():
                buf_out[row] = jnp.zeros((block, width), jnp.float32)

            pltpu.make_async_copy(
                buf_out.at[row], modes_ref.at[jnp.bitwise_and(slot, CAP - 1)], sem_out
            ).start()
        return carry

    lax.fori_loop(0, steps, step, 0)
    cross = jnp.concatenate([total[:, half + r, :] for r in range(half)], axis=0) / row_total
    operator_ref[...] = dot3(inverse_t, dot3(cross, inverse))
    pltpu.make_async_copy(buf_out, modes_ref, sem_out).wait()


def settle(arrived, row_total, block):
    count, _, width = arrived.shape
    anywhere = pl.BlockSpec(memory_space=pl.ANY)
    rows = pltpu.VMEM((count, block, width), jnp.float32)
    return pl.pallas_call(
        functools.partial(settle_kernel, float(row_total)),
        in_specs=[anywhere],
        out_specs=(anywhere, pl.BlockSpec(memory_space=pltpu.VMEM)),
        out_shape=(
            jax.ShapeDtypeStruct((count, block, width), jnp.float32),
            jax.ShapeDtypeStruct((width, width), jnp.float32),
        ),
        scratch_shapes=[
            rows,
            rows,
            pltpu.VMEM((count, SUM_ROWS, width), jnp.float32),
            pltpu.VMEM((width, 2 * width), jnp.float32),
            pltpu.VMEM((2 * width, 2 * width), jnp.bfloat16),
            pltpu.VMEM((1, count), jnp.int32),
            pltpu.SMEM((1, count), jnp.int32),
            pltpu.SemaphoreType.DMA,
            pltpu.SemaphoreType.DMA((count // APPLY_STEP,)),
            pltpu.SemaphoreType.DMA,
            pltpu.SemaphoreType.DMA,
        ],
        cost_estimate=pl.CostEstimate(
            flops=8 * count * block * width * width, bytes_accessed=1 << 23, transcendentals=0
        ),
        name="settle",
    )(arrived)


def exchange(payload, axes=AXES):
    return lax.all_to_all(payload, axes, split_axis=0, concat_axis=0, tiled=True)


def body(snap_early, snap_late, block_ids, block_owner, block_slot):
    members = lax.axis_size(AXES)
    count, block, width = snap_late.shape
    row_total = count * block * members
    outgoing = gram_pair(snap_early, snap_late)
    block_ids, outgoing = lax.optimization_barrier((block_ids, outgoing))
    partial = exchange(outgoing, PLANE)
    labels = jnp.arange(block_owner.shape[0], dtype=jnp.int32)
    code = block_owner * CAP + block_slot
    hits = block_ids[:, None] == labels[None, :]
    code_here = jnp.sum(jnp.where(hits, code[None, :], 0), axis=1)
    dest = code_here // CAP
    first = pack(snap_late, dest, members, 0, block, SUM_ROWS)
    arrived = exchange(mix(partial, code_here[None, :], first))
    modes, operator = settle(arrived, row_total, block)
    return (modes, operator)


def solution(mesh):
    split = jax.sharding.Mesh(mesh.devices.reshape((4, 4, 4, 2)), AXES)
    placed = (
        P(AXES, None, None),
        P(AXES, None, None),
        P(AXES),
        P(),
        P(),
    )
    return jax.shard_map(
        body,
        mesh=split,
        in_specs=placed,
        out_specs=(P(AXES, None, None), P()),
        check_vma=False,
    )
```

time: 162 us -> 157 us (0.969)
  blocking collectives: 0 us -> 113 us
  waiting for transfers between devices: 86.7 us -> 0.42 us
  starting transfers between devices: 28 us -> 9.43 us
  Pallas kernels: 44.3 us -> 30.7 us
    all_to_all x0 -> x1, blocking collectives: none -> 113 us  [exchange(): lax.all_to_all(payload, axes, split_axis=0, concat_axis=0, tiled=True)]
    all_to_all x3 -> x1, waiting for transfers between devices: 86.7 us -> 0.42 us  [exchange(): lax.all_to_all(payload, axes, split_axis=0, concat_axis=0, tiled=True)]
    all_to_all x3 -> x1, starting transfers between devices: 28 us -> 9.43 us  [exchange(): lax.all_to_all(payload, axes, split_axis=0, concat_axis=0, tiled=True)]
    pallas_call x3 -> x1, Pallas kernels: 28 us -> 15.7 us  [settle(): pl.pallas_call(functools.partial(settle_kernel, float(row_total)), in_spe...]
    pallas_call x2 -> x1, Pallas kernels: 7.22 us -> 5.87 us  [pack(): pl.pallas_call(functools.partial(pack_kernel, lo, height), grid_spec=pltp...]
  transfers between devices with their start and end apart: 3 -> 1, of which waited for: 3 -> 1; matrix products, arithmetic and copies ran while one was open for 1% -> 1% of each run, Pallas kernels for 20% -> 4%
where the time goes in v5:
time: 157 us
  blocking collectives  113 us (72%)
  Pallas kernels  30.7 us (20%)
  starting transfers between devices  9.43 us (6%)
    all_to_all x1, blocking collectives, exchange(): lax.all_to_all(payload, axes, split_axis=0, concat_axis=0, tiled=True)  113 us
    pallas_call x1, Pallas kernels, settle(): pl.pallas_call(functools.partial(settle_kernel, float(row_total)), in_spe...  15.7 us
    all_to_all x1, starting transfers between devices, exchange(): lax.all_to_all(payload, axes, split_axis=0, concat_axis=0, tiled=True)  9.43 us
    pallas_call x1, Pallas kernels, gram_pair(): pl.pallas_call(gram_kernel, in_specs=[anywhere, anywhere], out_specs=pl.B...  7.25 us
    pallas_call x1, Pallas kernels, pack(): pl.pallas_call(functools.partial(pack_kernel, lo, height), grid_spec=pltp...  5.87 us
  transfers between devices with their start and end apart: 1, of which 1 were waited for; matrix products, arithmetic and copies ran while one was open for 1% of the time, Pallas kernels for 4%

profile of v5, /device:TPU:1, one launch (start us, length us, event | category | flops | bytes accessed | tf_op | source)
XLA Modules:
  0.0 156.7 jit_solution(14821489085370130648)
XLA Ops:
  0.6 0.0 copy-start.4
  0.6 0.0 copy-start.1
  0.7 0.0 copy-start.2
  0.7 7.3 %gram.1 = f32[32,8,128]{2,1,0:T(8,128)} custom-call(f32[96,128,128]{2,1,0:T(8,128)} %early_ref.1, f32[96,128,128]{2,1,0:T(8,128)} %late_ref.3), custom_call_target="tpu_custom_call" | custom-call | flops 2415919104 | bytes 8388608 | tf_op jit(solution)/shard_map/gram/pallas_call | solution.py:118
  7.9 9.4 %all-to-all-start = ((f32[32,8,128]{2,1,0:T(8,128)}), f32[32,8,128]{2,1,0:T(8,128)S(1)}, u32[]{:S(2)}, u32[]{:S(2)}) async-start(f32[32,8,128]{2,1,0:T(8,128)} %gram.1), calls=%async_computation | async-start | bytes 262144 | tf_op jit(solution)/shard_map/all_to_all | solution.py:357
  17.4 0.0 copy-done.1
  17.4 0.0 copy-done.2
  17.4 0.0 copy-done.4
  17.4 0.8 select_reduce_fusion
  18.2 0.0 copy-start.3
  18.2 0.5 and_select_fusion.dest_ref
  18.7 5.9 %pack.1.first_ref = f32[128,136,128]{2,1,0:T(8,128)} custom-call(s32[96]{0:T(128)} %and_select_fusion.dest_ref, f32[96,128,128]{2,1,0:T(8,128)} %late_ref.3), custom_call_target="tpu_custom_call" | custom-call | flops 100000000 | bytes 8388608 | tf_op jit(solution)/shard_map/pack/pallas_call | solution.py:60
  24.6 0.0 copy-done.3
  24.6 0.4 all-to-all-done.partial_ref
  25.0 0.0 copy-start
  25.0 0.7 copy-done
  25.7 1.9 %mix.1 = f32[128,136,128]{2,1,0:T(8,128)} custom-call(f32[32,8,128]{2,1,0:T(8,128)} %copy-done, s32[1,96]{1,0:T(1,128)} %bitcast.1, f32[128,136,128]{2,1,0:T(8,128)} %pack.1.first_ref), custom_call_target="tpu_custom_call", output_to_operand_aliasing={{}: (2, {})} | custom-call | flops 1000000 | bytes 524288 | tf_op jit(solution)/shard_map/mix/pallas_call | solution.py:158
  27.6 113.4 %all_to_all.10.arrived_ref = f32[128,136,128]{2,1,0:T(8,128)} all-to-all(f32[128,136,128]{2,1,0:T(8,128)} %mix.1), channel_id=1, replica_groups=mesh['y'=4,'x'=4,'z'=4,'core'=2] {'y','x','z','core'}, dimensions={0} | all-to-all | bytes 17825792 | tf_op jit(solution)/shard_map/all_to_all | solution.py:357
  141.0 15.7 %settle.1 = (f32[128,128,128]{2,1,0:T(8,128)}, f32[128,128]{1,0:T(8,128)}) custom-call(f32[128,136,128]{2,1,0:T(8,128)} %all_to_all.10.arrived_ref), custom_call_target="tpu_custom_call" | custom-call | flops 2147483648 | bytes 8388608 | tf_op jit(solution)/shard_map/settle/pallas_call | solution.py:328
  (1 shorter events, 0.0 us)
Async XLA Ops:
  0.6 16.8 %copy-start.4 = (s32[96]{0:T(128)S(1)}, s32[96]{0:T(128)}, u32[]{:S(2)}) copy-start(s32[96]{0:T(128)} %param.7) | copy-start | bytes 1156
  0.6 16.7 %copy-start.1 = (s32[12288]{0:T(1024)S(1)}, s32[12288]{0:T(1024)}, u32[]{:S(2)}) copy-start(s32[12288]{0:T(1024)} %param.9) | copy-start | bytes 147460
  0.7 16.7 %copy-start.2 = (s32[12288]{0:T(1024)S(1)}, s32[12288]{0:T(1024)}, u32[]{:S(2)}) copy-start(s32[12288]{0:T(1024)} %param.8) | copy-start | bytes 147460
  7.9 17.1 %all-to-all-start = ((f32[32,8,128]{2,1,0:T(8,128)}), f32[32,8,128]{2,1,0:T(8,128)S(1)}, u32[]{:S(2)}, u32[]{:S(2)}) async-start(f32[32,8,128]{2,1,0:T(8,128)} %gram.1), calls=%async_computation | async-start | bytes 262144 | tf_op jit(solution)/shard_map/all_to_all | solution.py:357
  18.2 6.4 %copy-start.3 = (s32[96]{0:T(128)}, s32[96]{0:T(128)S(1)}, u32[]{:S(2)}) copy-start(s32[96]{0:T(128)S(1)} %select_reduce_fusion) | copy-start | bytes 1156
  25.0 0.7 copy-start

commit v6 on v5

--- a/solution.py
+++ b/solution.py
@@ -10,7 +10,6 @@
 AXES = ("y", "x", "z", "core")
 PLANE = ("x", "z", "core")
 GRAM_CHUNKS = (16, 32, 48)
-PACK_CHUNKS = 4
 APPLY_STEP = 16
 SUM_ROWS = 8
 PIVOTS = 4
@@ -30,54 +29,35 @@
     )
 
 
-def pack_kernel(lo, height, dest_ref, late_ref, out_ref, buf, sem_in, sem_out):
-    count = late_ref.shape[0]
-    size = count // PACK_CHUNKS
-    rows = pl.ds(0, height)
-
-    def load(t):
-        part = pl.ds(t * size, size)
-        return pltpu.make_async_copy(
-            late_ref.at[part, pl.ds(lo, height)], buf.at[part], sem_in.at[t]
-        )
-
-    for t in range(PACK_CHUNKS):
-        load(t).start()
-    for t in range(PACK_CHUNKS):
-        load(t).wait()
-
-        def send(i, carry):
-            pltpu.make_async_copy(buf.at[i], out_ref.at[dest_ref[i], rows], sem_out).start()
-            return carry
-
-        lax.fori_loop(t * size, t * size + size, send, 0, unroll=8)
-    pltpu.make_async_copy(buf, out_ref.at[pl.ds(0, count), rows], sem_out).wait()
-
-
-def pack(late, dest, members, lo, height, spare):
-    count, _, width = late.shape
-    anywhere = pl.BlockSpec(memory_space=pl.ANY)
-    return pl.pallas_call(
-        functools.partial(pack_kernel, lo, height),
-        grid_spec=pltpu.PrefetchScalarGridSpec(
-            num_scalar_prefetch=1,
-            grid=(1,),
-            in_specs=[anywhere],
-            out_specs=anywhere,
-            scratch_shapes=[
-                pltpu.VMEM((count, height, width), jnp.float32),
-                pltpu.SemaphoreType.DMA((PACK_CHUNKS,)),
-                pltpu.SemaphoreType.DMA,
-            ],
-        ),
-        out_shape=jax.ShapeDtypeStruct((members, height + spare, width), jnp.float32),
-        cost_estimate=pl.CostEstimate(flops=100000000, bytes_accessed=1 << 23, transcendentals=0),
-        name="pack",
-    )(dest, late)
-
-
-def gram_kernel(early_ref, late_ref, out_ref, early_buf, late_buf, sem_early, sem_late):
-    width = early_ref.shape[2]
+def gram_kernel(
+    early_ref,
+    late_ref,
+    ids_ref,
+    owner_ref,
+    slot_ref,
+    out_ref,
+    first_ref,
+    code_ref,
+    early_buf,
+    late_buf,
+    ids_buf,
+    owner_buf,
+    slot_buf,
+    code_buf,
+    code_now,
+    sem_early,
+    sem_late,
+    sem_table,
+    sem_code,
+    sem_out,
+):
+    count, block, width = late_ref.shape
+    tables = []
+    for k, (source, target) in enumerate(
+        ((ids_ref, ids_buf), (owner_ref, owner_buf), (slot_ref, slot_buf))
+    ):
+        tables.append(pltpu.make_async_copy(source, target, sem_table.at[k]))
+        tables[-1].start()
     parts = []
     lo = 0
     for k, size in enumerate(GRAM_CHUNKS):
@@ -86,12 +66,44 @@
         two = pltpu.make_async_copy(late_ref.at[part], late_buf.at[part], sem_late.at[k])
         one.start()
         two.start()
-        parts.append((part, one, two))
+        parts.append((lo, size, one, two))
         lo += size
+
+    for copy in tables:
+        copy.wait()
+    ids = ids_buf[...]
+    lines, lanes = owner_buf.shape
+    line_id = lax.broadcasted_iota(jnp.int32, (lines, count), 0)
+    lane_id = lax.broadcasted_iota(jnp.int32, (lanes, count), 0)
+    line = (line_id == jnp.right_shift(ids, 7)).astype(jnp.float32).astype(jnp.bfloat16)
+    table = jnp.concatenate([owner_buf[...], slot_buf[...]], axis=1)
+    found = contract_rows(table.astype(jnp.float32).astype(jnp.bfloat16), line)
+    here = lane_id == jnp.bitwise_and(ids, lanes - 1)
+    owner = jnp.sum(jnp.where(here, found[0:lanes], 0.0), axis=0, keepdims=True)
+    slot = jnp.sum(jnp.where(here, found[lanes:], 0.0), axis=0, keepdims=True)
+    code = (owner * CAP + slot).astype(jnp.int32)
+    code_ref[...] = code
+    code_buf[...] = jnp.zeros_like(code_buf)
+    code_buf[:, 0:count] = code
+    code_copy = pltpu.make_async_copy(code_buf, code_now, sem_code)
+    code_copy.start()
+
     gram_wide = cross_wide = None
-    for part, one, two in parts:
+    for k, (lo, size, one, two) in enumerate(parts):
+        two.wait()
+        if k == 0:
+            code_copy.wait()
+
+        def send(i, carry):
+            peer = jnp.right_shift(code_now[0, i], 7)
+            pltpu.make_async_copy(
+                late_buf.at[i], first_ref.at[peer, pl.ds(0, block)], sem_out
+            ).start()
+            return carry
+
+        lax.fori_loop(lo, lo + size, send, 0, unroll=8)
         one.wait()
-        two.wait()
+        part = pl.ds(lo, size)
         ehi, elo = split_pair(early_buf[part].reshape((-1, width)))
         lhi, llo = split_pair(late_buf[part].reshape((-1, width)))
         pair = jnp.concatenate([ehi, elo], axis=1)
@@ -109,28 +121,44 @@
     for r in range(half):
         out_ref[:, r, :] = gram[r * size : (r + 1) * size, :]
         out_ref[:, half + r, :] = cross[r * size : (r + 1) * size, :]
-
-
-def gram_pair(early, late):
-    count, block, width = early.shape
+    pltpu.make_async_copy(
+        late_buf, first_ref.at[pl.ds(0, count), pl.ds(0, block)], sem_out
+    ).wait()
+
+
+def gram_and_pack(early, late, ids, owner, slot, members):
+    count, block, width = late.shape
     steps = len(GRAM_CHUNKS)
     anywhere = pl.BlockSpec(memory_space=pl.ANY)
+    whole = pl.BlockSpec(memory_space=pltpu.VMEM)
     return pl.pallas_call(
         gram_kernel,
-        in_specs=[anywhere, anywhere],
-        out_specs=pl.BlockSpec(memory_space=pltpu.VMEM),
-        out_shape=jax.ShapeDtypeStruct((2 * width // SUM_ROWS, SUM_ROWS, width), jnp.float32),
+        in_specs=[anywhere] * 5,
+        out_specs=(whole, anywhere, whole),
+        out_shape=(
+            jax.ShapeDtypeStruct((2 * width // SUM_ROWS, SUM_ROWS, width), jnp.float32),
+            jax.ShapeDtypeStruct((members, block + SUM_ROWS, width), jnp.float32),
+            jax.ShapeDtypeStruct((1, count), jnp.int32),
+        ),
         scratch_shapes=[
             pltpu.VMEM((count, block, width), jnp.float32),
             pltpu.VMEM((count, block, width), jnp.float32),
+            pltpu.VMEM(ids.shape, jnp.int32),
+            pltpu.VMEM(owner.shape, jnp.int32),
+            pltpu.VMEM(slot.shape, jnp.int32),
+            pltpu.VMEM((1, CAP), jnp.int32),
+            pltpu.SMEM((1, CAP), jnp.int32),
             pltpu.SemaphoreType.DMA((steps,)),
             pltpu.SemaphoreType.DMA((steps,)),
+            pltpu.SemaphoreType.DMA((3,)),
+            pltpu.SemaphoreType.DMA,
+            pltpu.SemaphoreType.DMA,
         ],
         cost_estimate=pl.CostEstimate(
             flops=12 * count * block * width * width, bytes_accessed=1 << 23, transcendentals=0
         ),
         name="gram",
-    )(early, late)
+    )(early, late, ids, owner, slot)
 
 
 def mix_kernel(partial_ref, code_ref, first_ref, out_ref, rows, sem):
@@ -175,13 +203,14 @@
     return jnp.dot(a, b, precision=lax.Precision.HIGHEST, preferred_element_type=jnp.float32)
 
 
-def eliminate(work):
+def eliminate(work, beside):
     order = work.shape[0]
     lane = lax.broadcasted_iota(jnp.int32, (1, 2 * order), 1)
     lane_half = lax.broadcasted_iota(jnp.int32, (1, order), 1)
 
     def step(lo, k, carry):
         j = lo + k * PIVOTS
+        beside(lo // PIVOTS + k)
         row_id = lo + lax.broadcasted_iota(jnp.int32, (order - lo, 1), 0)
         table = work[lo:order, :]
         left = table[:, 0:order]
@@ -230,6 +259,7 @@
     modes_ref,
     operator_ref,
     buf_in,
+    pairs,
     buf_out,
     stats_ref,
     work,
@@ -249,14 +279,21 @@
     )
     stats_copy.start()
 
-    def fetch(t):
-        part = pl.ds(t * APPLY_STEP, APPLY_STEP)
+    group = count * PIVOTS // order
+
+    def fetch(k):
+        part = pl.ds(k * group, group)
         return pltpu.make_async_copy(
-            arrived_ref.at[part, pl.ds(0, block)], buf_in.at[part], sem_in.at[t]
+            arrived_ref.at[part, pl.ds(0, block)], buf_in.at[part], sem_in.at[k]
         )
 
-    for t in range(steps):
-        fetch(t).start()
+    def divide(k):
+        fetch(k).wait()
+        rows = buf_in[pl.ds(k * group, group)].reshape((group * block, width))
+        pairs[k] = jnp.concatenate(split_pair(rows), axis=1)
+
+    for k in range(count // group):
+        fetch(k).start()
     stats_copy.wait()
 
     row_id = lax.broadcasted_iota(jnp.int32, (order, 1), 0)
@@ -281,7 +318,7 @@
     place_copy = pltpu.make_async_copy(place_ref, slots_ref, sem_place)
     place_copy.start()
 
-    eliminate(work)
+    eliminate(work, divide)
     inverse_t = work[:, order:]
     inverse = inverse_t.T
     whi, wlo = split_pair(inverse)
@@ -293,13 +330,9 @@
 
     def step(t, carry):
         part = pl.ds(t * APPLY_STEP, APPLY_STEP)
-        fetch(t).wait()
-        hi, low = split_pair(buf_in[part].reshape((APPLY_STEP * block, width)))
-        wide = jnp.dot(
-            jnp.concatenate([hi, low], axis=1),
-            weight_ref[...],
-            preferred_element_type=jnp.float32,
-        )
+        groups = APPLY_STEP // group
+        rows = pairs[pl.ds(t * groups, groups)].reshape((APPLY_STEP * block, 2 * width))
+        wide = jnp.dot(rows, weight_ref[...], preferred_element_type=jnp.float32)
         solved = wide[:, 0:width] + wide[:, width:]
         buf_out[part] = solved.reshape((APPLY_STEP, block, width))
         for i in range(APPLY_STEP):
@@ -325,6 +358,7 @@
     count, _, width = arrived.shape
     anywhere = pl.BlockSpec(memory_space=pl.ANY)
     rows = pltpu.VMEM((count, block, width), jnp.float32)
+    groups = width // PIVOTS
     return pl.pallas_call(
         functools.partial(settle_kernel, float(row_total)),
         in_specs=[anywhere],
@@ -335,6 +369,7 @@
         ),
         scratch_shapes=[
             rows,
+            pltpu.VMEM((groups, count * block // groups, 2 * width), jnp.bfloat16),
             rows,
             pltpu.VMEM((count, SUM_ROWS, width), jnp.float32),
             pltpu.VMEM((width, 2 * width), jnp.float32),
@@ -342,7 +377,7 @@
             pltpu.VMEM((1, count), jnp.int32),
             pltpu.SMEM((1, count), jnp.int32),
             pltpu.SemaphoreType.DMA,
-            pltpu.SemaphoreType.DMA((count // APPLY_STEP,)),
+            pltpu.SemaphoreType.DMA((groups,)),
             pltpu.SemaphoreType.DMA,
             pltpu.SemaphoreType.DMA,
         ],
@@ -359,18 +394,18 @@
 
 def body(snap_early, snap_late, block_ids, block_owner, block_slot):
     members = lax.axis_size(AXES)
-    count, block, width = snap_late.shape
+    count, block, _ = snap_late.shape
     row_total = count * block * members
-    outgoing = gram_pair(snap_early, snap_late)
-    block_ids, outgoing = lax.optimization_barrier((block_ids, outgoing))
+    outgoing, first, code = gram_and_pack(
+        snap_early,
+        snap_late,
+        block_ids.reshape((1, count)),
+        block_owner.reshape((-1, CAP)),
+        block_slot.reshape((-1, CAP)),
+        members,
+    )
     partial = exchange(outgoing, PLANE)
-    labels = jnp.arange(block_owner.shape[0], dtype=jnp.int32)
-    code = block_owner * CAP + block_slot
-    hits = block_ids[:, None] == labels[None, :]
-    code_here = jnp.sum(jnp.where(hits, code[None, :], 0), axis=1)
-    dest = code_here // CAP
-    first = pack(snap_late, dest, members, 0, block, SUM_ROWS)
-    arrived = exchange(mix(partial, code_here[None, :], first))
+    arrived = exchange(mix(partial, code, first))
     modes, operator = settle(arrived, row_total, block)
     return (modes, operator)
 

time: 157 us -> 156 us (level)
  blocking collectives: 113 us -> 127 us
  starting transfers between devices: 9.43 us -> 0 us
  Pallas kernels: 30.7 us -> 27.8 us
    all_to_all x1 -> x2, blocking collectives: 113 us -> 127 us  [exchange(): lax.all_to_all(payload, axes, split_axis=0, concat_axis=0, tiled=True)]
    all_to_all x1 -> x0, starting transfers between devices: 9.43 us -> none  [exchange(): lax.all_to_all(payload, axes, split_axis=0, concat_axis=0, tiled=True)]
    pallas_call x2 -> x1, Pallas kernels: 13.1 us -> 8.32 us  [gram_and_pack(): pl.pallas_call(gram_kernel, in_specs=[anywhere] * 5, out_specs=(whole, an...]
    pallas_call x1, Pallas kernels: 15.7 us -> 17.6 us  [settle(): pl.pallas_call(functools.partial(settle_kernel, float(row_total)), in_spe...]
  transfers between devices with their start and end apart: 1 -> 0, of which waited for: 1 -> 0; matrix products, arithmetic and copies ran while one was open for 1% -> 0% of each run, Pallas kernels for 4% -> 0%
where the time goes in v6:
time: 156 us
  blocking collectives  127 us (81%)
  Pallas kernels  27.8 us (18%)
    all_to_all x2, blocking collectives, exchange(): lax.all_to_all(payload, axes, split_axis=0, concat_axis=0, tiled=True)  127 us
    pallas_call x1, Pallas kernels, settle(): pl.pallas_call(functools.partial(settle_kernel, float(row_total)), in_spe...  17.6 us
    pallas_call x1, Pallas kernels, gram_and_pack(): pl.pallas_call(gram_kernel, in_specs=[anywhere] * 5, out_specs=(whole, an...  8.32 us

profile of v6, /device:TPU:1, one launch (start us, length us, event | category | flops | bytes accessed | tf_op | source)
XLA Modules:
  0.0 155.9 jit_solution(8230787158395568755)
XLA Ops:
  0.6 8.3 %gram.1 = (f32[32,8,128]{2,1,0:T(8,128)}, f32[128,136,128]{2,1,0:T(8,128)}, s32[1,96]{1,0:T(1,128)}) custom-call(f32[96,128,128]{2,1,0:T(8,128)} %early_ref.1, f32[96,128,128]{2,1,0:T(8,128)} %late_ref.1, s32[1,96]{1,0:T(1,128)} %bitcast.5, s32[96,128]{1,0:T(8,128)} %bitcast.3, s32[96,128]{1,0:T(8,128)} %bitcast.4), custom_call_target="tpu_custom_call" | custom-call | flops 2415919104 | bytes 8388608 | tf_op jit(solution)/shard_map/gram/pallas_call | solution.py:134
  9.0 17.2 %all_to_all.10.partial_ref = f32[32,8,128]{2,1,0:T(8,128)} all-to-all(f32[32,8,128]{2,1,0:T(8,128)} %get-tuple-element.5), channel_id=1, replica_groups=mesh['y'=4,'x'=4,'z'=4,'core'=2] {'x','z','core'}, dimensions={0} | all-to-all | bytes 262144 | tf_op jit(solution)/shard_map/all_to_all | solution.py:392
  26.2 1.9 %mix.1 = f32[128,136,128]{2,1,0:T(8,128)} custom-call(f32[32,8,128]{2,1,0:T(8,128)} %all_to_all.10.partial_ref, s32[1,96]{1,0:T(1,128)} %get-tuple-element.6.code_ref, f32[128,136,128]{2,1,0:T(8,128)} %get-tuple-element.7.first_ref), custom_call_target="tpu_custom_call", output_to_operand_aliasing={{}: (2, {})} | custom-call | flops 1000000 | bytes 524288 | tf_op jit(solution)/shard_map/mix/pallas_call | solution.py:186
  28.1 110.2 %all_to_all.11.arrived_ref = f32[128,136,128]{2,1,0:T(8,128)} all-to-all(f32[128,136,128]{2,1,0:T(8,128)} %mix.1), channel_id=1, replica_groups=mesh['y'=4,'x'=4,'z'=4,'core'=2] {'y','x','z','core'}, dimensions={0} | all-to-all | bytes 17825792 | tf_op jit(solution)/shard_map/all_to_all | solution.py:392
  138.3 17.6 %settle.1 = (f32[128,128,128]{2,1,0:T(8,128)}, f32[128,128]{1,0:T(8,128)}) custom-call(f32[128,136,128]{2,1,0:T(8,128)} %all_to_all.11.arrived_ref), custom_call_target="tpu_custom_call" | custom-call | flops 2147483648 | bytes 8388608 | tf_op jit(solution)/shard_map/settle/pallas_call | solution.py:362

commit v7 on v6

--- a/solution.py
+++ b/solution.py
@@ -10,10 +10,10 @@
 AXES = ("y", "x", "z", "core")
 PLANE = ("x", "z", "core")
 GRAM_CHUNKS = (16, 32, 48)
-APPLY_STEP = 16
+APPLY_STEP = 64
 SUM_ROWS = 8
 PIVOTS = 4
-SHRINK = 32
+SHRINK = 16
 CAP = 128
 
 
@@ -203,14 +203,13 @@
     return jnp.dot(a, b, precision=lax.Precision.HIGHEST, preferred_element_type=jnp.float32)
 
 
-def eliminate(work, beside):
+def eliminate(work):
     order = work.shape[0]
     lane = lax.broadcasted_iota(jnp.int32, (1, 2 * order), 1)
     lane_half = lax.broadcasted_iota(jnp.int32, (1, order), 1)
 
     def step(lo, k, carry):
         j = lo + k * PIVOTS
-        beside(lo // PIVOTS + k)
         row_id = lo + lax.broadcasted_iota(jnp.int32, (order - lo, 1), 0)
         table = work[lo:order, :]
         left = table[:, 0:order]
@@ -259,7 +258,6 @@
     modes_ref,
     operator_ref,
     buf_in,
-    pairs,
     buf_out,
     stats_ref,
     work,
@@ -279,21 +277,14 @@
     )
     stats_copy.start()
 
-    group = count * PIVOTS // order
-
-    def fetch(k):
-        part = pl.ds(k * group, group)
+    def fetch(t):
+        part = pl.ds(t * APPLY_STEP, APPLY_STEP)
         return pltpu.make_async_copy(
-            arrived_ref.at[part, pl.ds(0, block)], buf_in.at[part], sem_in.at[k]
+            arrived_ref.at[part, pl.ds(0, block)], buf_in.at[part], sem_in.at[t]
         )
 
-    def divide(k):
-        fetch(k).wait()
-        rows = buf_in[pl.ds(k * group, group)].reshape((group * block, width))
-        pairs[k] = jnp.concatenate(split_pair(rows), axis=1)
-
-    for k in range(count // group):
-        fetch(k).start()
+    for t in range(steps):
+        fetch(t).start()
     stats_copy.wait()
 
     row_id = lax.broadcasted_iota(jnp.int32, (order, 1), 0)
@@ -318,7 +309,7 @@
     place_copy = pltpu.make_async_copy(place_ref, slots_ref, sem_place)
     place_copy.start()
 
-    eliminate(work, divide)
+    eliminate(work)
     inverse_t = work[:, order:]
     inverse = inverse_t.T
     whi, wlo = split_pair(inverse)
@@ -330,9 +321,13 @@
 
     def step(t, carry):
         part = pl.ds(t * APPLY_STEP, APPLY_STEP)
-        groups = APPLY_STEP // group
-        rows = pairs[pl.ds(t * groups, groups)].reshape((APPLY_STEP * block, 2 * width))
-        wide = jnp.dot(rows, weight_ref[...], preferred_element_type=jnp.float32)
+        fetch(t).wait()
+        hi, low = split_pair(buf_in[part].reshape((APPLY_STEP * block, width)))
+        wide = jnp.dot(
+            jnp.concatenate([hi, low], axis=1),
+            weight_ref[...],
+            preferred_element_type=jnp.float32,
+        )
         solved = wide[:, 0:width] + wide[:, width:]
         buf_out[part] = solved.reshape((APPLY_STEP, block, width))
         for i in range(APPLY_STEP):
@@ -358,7 +353,6 @@
     count, _, width = arrived.shape
     anywhere = pl.BlockSpec(memory_space=pl.ANY)
     rows = pltpu.VMEM((count, block, width), jnp.float32)
-    groups = width // PIVOTS
     return pl.pallas_call(
         functools.partial(settle_kernel, float(row_total)),
         in_specs=[anywhere],
@@ -369,7 +363,6 @@
         ),
         scratch_shapes=[
             rows,
-            pltpu.VMEM((groups, count * block // groups, 2 * width), jnp.bfloat16),
             rows,
             pltpu.VMEM((count, SUM_ROWS, width), jnp.float32),
             pltpu.VMEM((width, 2 * width), jnp.float32),
@@ -377,7 +370,7 @@
             pltpu.VMEM((1, count), jnp.int32),
             pltpu.SMEM((1, count), jnp.int32),
             pltpu.SemaphoreType.DMA,
-            pltpu.SemaphoreType.DMA((groups,)),
+            pltpu.SemaphoreType.DMA((count // APPLY_STEP,)),
             pltpu.SemaphoreType.DMA,
             pltpu.SemaphoreType.DMA,
         ],

time: 156 us -> 152 us (0.974)
  Pallas kernels: 27.8 us -> 24.1 us
    pallas_call x1, Pallas kernels: 17.6 us -> 13.9 us  [settle(): pl.pallas_call(functools.partial(settle_kernel, float(row_total)), in_spe...]
where the time goes in v7:
time: 152 us
  blocking collectives  127 us (84%)
  Pallas kernels  24.1 us (16%)
    all_to_all x2, blocking collectives, exchange(): lax.all_to_all(payload, axes, split_axis=0, concat_axis=0, tiled=True)  127 us
    pallas_call x1, Pallas kernels, settle(): pl.pallas_call(functools.partial(settle_kernel, float(row_total)), in_spe...  13.9 us
    pallas_call x1, Pallas kernels, gram_and_pack(): pl.pallas_call(gram_kernel, in_specs=[anywhere] * 5, out_specs=(whole, an...  8.32 us

profile of v7, /device:TPU:1, one launch (start us, length us, event | category | flops | bytes accessed | tf_op | source)
XLA Modules:
  0.0 152.2 jit_solution(7848582743714740212)
XLA Ops:
  0.6 8.3 %gram.1 = (f32[32,8,128]{2,1,0:T(8,128)}, f32[128,136,128]{2,1,0:T(8,128)}, s32[1,96]{1,0:T(1,128)}) custom-call(f32[96,128,128]{2,1,0:T(8,128)} %early_ref.1, f32[96,128,128]{2,1,0:T(8,128)} %late_ref.1, s32[1,96]{1,0:T(1,128)} %bitcast.5, s32[96,128]{1,0:T(8,128)} %bitcast.3, s32[96,128]{1,0:T(8,128)} %bitcast.4), custom_call_target="tpu_custom_call" | custom-call | flops 2415919104 | bytes 8388608 | tf_op jit(solution)/shard_map/gram/pallas_call | solution.py:134
  9.0 17.2 %all_to_all.10.partial_ref = f32[32,8,128]{2,1,0:T(8,128)} all-to-all(f32[32,8,128]{2,1,0:T(8,128)} %get-tuple-element.5), channel_id=1, replica_groups=mesh['y'=4,'x'=4,'z'=4,'core'=2] {'x','z','core'}, dimensions={0} | all-to-all | bytes 262144 | tf_op jit(solution)/shard_map/all_to_all | solution.py:385
  26.2 1.9 %mix.1 = f32[128,136,128]{2,1,0:T(8,128)} custom-call(f32[32,8,128]{2,1,0:T(8,128)} %all_to_all.10.partial_ref, s32[1,96]{1,0:T(1,128)} %get-tuple-element.6.code_ref, f32[128,136,128]{2,1,0:T(8,128)} %get-tuple-element.7.first_ref), custom_call_target="tpu_custom_call", output_to_operand_aliasing={{}: (2, {})} | custom-call | flops 1000000 | bytes 524288 | tf_op jit(solution)/shard_map/mix/pallas_call | solution.py:186
  28.1 110.2 %all_to_all.11.arrived_ref = f32[128,136,128]{2,1,0:T(8,128)} all-to-all(f32[128,136,128]{2,1,0:T(8,128)} %mix.1), channel_id=1, replica_groups=mesh['y'=4,'x'=4,'z'=4,'core'=2] {'y','x','z','core'}, dimensions={0} | all-to-all | bytes 17825792 | tf_op jit(solution)/shard_map/all_to_all | solution.py:385
  138.3 13.9 %settle.1 = (f32[128,128,128]{2,1,0:T(8,128)}, f32[128,128]{1,0:T(8,128)}) custom-call(f32[128,136,128]{2,1,0:T(8,128)} %all_to_all.11.arrived_ref), custom_call_target="tpu_custom_call" | custom-call | flops 2147483648 | bytes 8388608 | tf_op jit(solution)/shard_map/settle/pallas_call | solution.py:356

commit v8 on v7

--- a/solution.py
+++ b/solution.py
@@ -13,7 +13,7 @@
 APPLY_STEP = 64
 SUM_ROWS = 8
 PIVOTS = 4
-SHRINK = 16
+SHRINK = 8
 CAP = 128
 
 
@@ -161,12 +161,15 @@
     )(early, late, ids, owner, slot)
 
 
-def mix_kernel(partial_ref, code_ref, first_ref, out_ref, rows, sem):
+def mix_kernel(partial_ref, code_ref, first_ref, out_ref, rows, code_buf, sem, sem_code):
     members, _, width = rows.shape
+    code_copy = pltpu.make_async_copy(code_ref, code_buf, sem_code)
+    code_copy.start()
     total = jnp.sum(partial_ref[...], axis=0, keepdims=True)
     rows[...] = jnp.broadcast_to(total, rows.shape)
     mark = SUM_ROWS // 2 - 1
-    code = code_ref[...]
+    code_copy.wait()
+    code = code_buf[...]
     peer = lax.broadcasted_iota(jnp.int32, (members, code.shape[1]), 0)
     slot = (jnp.bitwise_and(code, CAP - 1) + 1).astype(jnp.float32)
     here = jnp.where(jnp.right_shift(code, 7) == peer, slot, 0.0)
@@ -185,16 +188,18 @@
     anywhere = pl.BlockSpec(memory_space=pl.ANY)
     return pl.pallas_call(
         mix_kernel,
-        in_specs=[whole, whole, anywhere],
+        in_specs=[whole, anywhere, anywhere],
         out_specs=anywhere,
         out_shape=jax.ShapeDtypeStruct(first.shape, first.dtype),
         scratch_shapes=[
             pltpu.VMEM((members, SUM_ROWS, width), jnp.float32),
+            pltpu.VMEM(code.shape, jnp.int32),
+            pltpu.SemaphoreType.DMA,
             pltpu.SemaphoreType.DMA,
         ],
         input_output_aliases={2: 0},
         cost_estimate=pl.CostEstimate(flops=1000000, bytes_accessed=1 << 19, transcendentals=0),
-        compiler_params=pltpu.CompilerParams(vmem_limit_bytes=57 << 20),
+        compiler_params=pltpu.CompilerParams(vmem_limit_bytes=52 << 20),
         name="mix",
     )(partial, code, first)
 
@@ -285,6 +290,7 @@
 
     for t in range(steps):
         fetch(t).start()
+    buf_out[count] = jnp.zeros((block, width), jnp.float32)
     stats_copy.wait()
 
     row_id = lax.broadcasted_iota(jnp.int32, (order, 1), 0)
@@ -333,20 +339,16 @@
         for i in range(APPLY_STEP):
             row = t * APPLY_STEP + i
             slot = slots_ref[0, row]
-
-            @pl.when(slot >= CAP)
-            def _():
-                buf_out[row] = jnp.zeros((block, width), jnp.float32)
-
+            source = jnp.where(slot >= CAP, count, row)
             pltpu.make_async_copy(
-                buf_out.at[row], modes_ref.at[jnp.bitwise_and(slot, CAP - 1)], sem_out
+                buf_out.at[source], modes_ref.at[jnp.bitwise_and(slot, CAP - 1)], sem_out
             ).start()
         return carry
 
     lax.fori_loop(0, steps, step, 0)
     cross = jnp.concatenate([total[:, half + r, :] for r in range(half)], axis=0) / row_total
     operator_ref[...] = dot3(inverse_t, dot3(cross, inverse))
-    pltpu.make_async_copy(buf_out, modes_ref, sem_out).wait()
+    pltpu.make_async_copy(buf_out.at[pl.ds(0, count)], modes_ref, sem_out).wait()
 
 
 def settle(arrived, row_total, block):
@@ -363,7 +365,7 @@
         ),
         scratch_shapes=[
             rows,
-            rows,
+            pltpu.VMEM((count + 1, block, width), jnp.float32),
             pltpu.VMEM((count, SUM_ROWS, width), jnp.float32),
             pltpu.VMEM((width, 2 * width), jnp.float32),
             pltpu.VMEM((2 * width, 2 * width), jnp.bfloat16),

time: 152 us -> 152 us (level)
  no operation moved by 1% of the time
where the time goes in v8:
time: 152 us; the launch traced here: 151 us
  blocking collectives  127 us (84%)
  Pallas kernels  22.7 us (15%)
    all_to_all x2, blocking collectives, exchange(): lax.all_to_all(payload, axes, split_axis=0, concat_axis=0, tiled=True)  127 us
    pallas_call x1, Pallas kernels, settle(): pl.pallas_call(functools.partial(settle_kernel, float(row_total)), in_spe...  13.3 us
    pallas_call x1, Pallas kernels, gram_and_pack(): pl.pallas_call(gram_kernel, in_specs=[anywhere] * 5, out_specs=(whole, an...  8.32 us

profile of v8, /device:TPU:1, one launch (start us, length us, event | category | flops | bytes accessed | tf_op | source)
XLA Modules:
  0.0 151.3 jit_solution(16754984084912227773)
XLA Ops:
  0.6 8.3 %gram.1 = (f32[32,8,128]{2,1,0:T(8,128)}, f32[128,136,128]{2,1,0:T(8,128)}, s32[1,96]{1,0:T(1,128)}) custom-call(f32[96,128,128]{2,1,0:T(8,128)} %early_ref.1, f32[96,128,128]{2,1,0:T(8,128)} %late_ref.1, s32[1,96]{1,0:T(1,128)} %bitcast.5, s32[96,128]{1,0:T(8,128)} %bitcast.3, s32[96,128]{1,0:T(8,128)} %bitcast.4), custom_call_target="tpu_custom_call" | custom-call | flops 2415919104 | bytes 8388608 | tf_op jit(solution)/shard_map/gram/pallas_call | solution.py:134
  9.0 17.1 %all_to_all.10.partial_ref = f32[32,8,128]{2,1,0:T(8,128)S(1)} all-to-all(f32[32,8,128]{2,1,0:T(8,128)} %get-tuple-element.5), channel_id=1, replica_groups=mesh['y'=4,'x'=4,'z'=4,'core'=2] {'x','z','core'}, dimensions={0} | all-to-all | bytes 262144 | tf_op jit(solution)/shard_map/all_to_all | solution.py:387
  26.1 0.0 copy-start
  26.1 0.7 copy-done
  26.7 1.1 mix.1
  27.8 110.2 %all_to_all.11.arrived_ref = f32[128,136,128]{2,1,0:T(8,128)} all-to-all(f32[128,136,128]{2,1,0:T(8,128)} %mix.1), channel_id=1, replica_groups=mesh['y'=4,'x'=4,'z'=4,'core'=2] {'y','x','z','core'}, dimensions={0} | all-to-all | bytes 17825792 | tf_op jit(solution)/shard_map/all_to_all | solution.py:387
  138.0 13.3 %settle.1 = (f32[128,128,128]{2,1,0:T(8,128)}, f32[128,128]{1,0:T(8,128)}) custom-call(f32[128,136,128]{2,1,0:T(8,128)} %all_to_all.11.arrived_ref), custom_call_target="tpu_custom_call" | custom-call | flops 2147483648 | bytes 8388608 | tf_op jit(solution)/shard_map/settle/pallas_call | solution.py:358
Async XLA Ops:
  26.1 0.7 copy-start
